TPU v7x, 32 devices: a whole 2x2x4 slice. The times are simulated.
32 devices in a mesh: dp: 8 (over z, y), mp: 4 (over x, core).
Axes of the slice: x: 2, y: 2, z: 4, core: 2. Of those that a mesh axis runs over, the one named last changes fastest.
Arguments:
- features: bfloat16 [3, 512, 16384], P(None, 'mp', 'dp'), may hold values from -6 to 6
- weights: bfloat16 [11, 512, 512], P(None, 'mp'), may hold values from -0.25 to 0.25
- sample_owner: int32 [3, 16384, 1], P(None, 'dp'), may hold values from 0 to 7; in each aligned block of 2048 rows (0 to 2047, 2048 to 4095, ..., all dimensions but the last counted through in order) at most 512 rows name the same one
- sample_row: int32 [3, 16384], P(None, 'dp'), may hold values from 0 to 2047
- edge_src: int32 [8, 16384], P(None, 'dp'), may hold values from 0 to 2047
- edge_dst: int32 [8, 16384], P(None, 'dp'), may hold values from 0 to 127
- edge_count: int32 [8, 8], P(None, 'dp'), may hold values from 128 to 2048
Outputs:
- updated: bfloat16 [3, 512, 1024], P(None, 'mp', 'dp')
Inputs may be any that keep to these rules, and one draw needn't show every extreme that they name: `sample_owner`: among the 2048 entries of one node type in one block no owner appears more than 512 times; some owner appears exactly 512 times in some blocks.
All inputs are finite; a program needn't handle non-finite values.
Results may differ from a plain program's by a relative error of at most 0.0064.
Values may be sent and summed in bfloat16 or wider, within the bound.
A program may use at most 64 MiB of HBM per device.

v0:
```python
import functools

import jax
import jax.numpy as jnp
from jax import lax
from jax.experimental import pallas as pl
from jax.experimental.pallas import tpu as pltpu
from jax.sharding import PartitionSpec as P

SEEDS = 128
RELATION_SOURCE = (0, 1, 0, 1, 2, 0, 2, 1)
MATRIX_TARGET = (1, 0, 0, 2, 1, 2, 0, 1, 0, 1, 2)
RELS = len(RELATION_SOURCE)
KINDS = 3
MATS = RELS + KINDS
SLOTS = tuple(
    tuple([r for r in range(RELS) if RELATION_SOURCE[r] == k] + [RELS + k]) for k in range(KINDS)
)
ORDER = tuple(m for group in SLOTS for m in group)
STARTS = tuple(sum(len(group) for group in SLOTS[:k]) for k in range(KINDS))
RELATIONS = tuple(m for m in ORDER if m < RELS)
HALVES = 2
CORES = 2
STEP = 256
MESH = pl.DeviceIdType.MESH
NT = (((1,), (1,)), ((), ()))
TN = (((0,), (0,)), ((), ()))


def log2(n):
    return n.bit_length() - 1


def kernel(groups, shares, features_in, weights_in, owner, row, src, dst, count, out,
           features, weights, in_sem, iota, tab, req_send, req_recv, pos, edges, send, recv, adj, deg, part,
           part_send, part_recv, typed, typed_send, typed_recv,
           req_ss, req_rs, idx_ss, idx_rs, row_ss, row_rs, part_ss, part_rs, typed_ss, typed_rs, adj_ss, adj_rs):
    kinds, feat, rows = features.shape
    sampled = row.shape[1]
    edge_total = src.shape[1]
    cap = req_send.shape[2]
    low = tab.shape[2]
    share = RELS // CORES
    high = rows // low
    s_high = sampled // low
    side = groups // HALVES
    g = lax.axis_index("dp")
    m = lax.axis_index("mp")
    half = g // side
    q = lax.rem(g, side)
    core = lax.rem(m, CORES)
    f32, bf16, i32 = jnp.float32, jnp.bfloat16, jnp.int32

    def one_hot(index, size):
        n = index.shape[1]
        pieces = []
        for base in range(0, size, STEP):
            span = min(STEP, size - base)
            local = index - base
            local = jnp.where((local >= 0) & (local < span), local, -1).astype(f32).astype(bf16)
            hit = iota[:span, :n] == local
            pieces.append(jnp.where(hit, jnp.ones((), bf16), jnp.zeros((), bf16)))
        return pieces[0] if len(pieces) == 1 else jnp.concatenate(pieces, axis=0)

    load_features = pltpu.make_async_copy(features_in, features, in_sem.at[0])
    load_weights = pltpu.make_async_copy(weights_in, weights, in_sem.at[1])
    load_features.start()
    load_weights.start()
    barrier = pltpu.get_barrier_semaphore()
    for d in range(1, groups):
        pl.semaphore_signal(barrier, inc=1, device_id={"dp": lax.rem(g + d, groups)}, device_id_type=MESH)
    for d in range(1, shares):
        pl.semaphore_signal(barrier, inc=1, device_id={"mp": lax.rem(m + d, shares)}, device_id_type=MESH)

    iota[...] = lax.broadcasted_iota(i32, iota.shape, 0).astype(f32).astype(bf16)
    tri = (lax.broadcasted_iota(i32, (STEP, STEP), 0) <= lax.broadcasted_iota(i32, (STEP, STEP), 1))
    tri = jnp.where(tri, 1.0, 0.0).astype(bf16)
    hot = jnp.concatenate([
        jnp.where(lax.broadcasted_iota(i32, (groups, sampled), 0) == owner[k], 1.0, 0.0)
        for k in range(kinds)], axis=0)
    lines = kinds * groups
    pieces = [hot[:, base:base + STEP] for base in range(0, sampled, STEP)]
    upto = jnp.dot(jnp.concatenate(pieces, axis=0).astype(bf16), tri, preferred_element_type=f32)
    carry = jnp.zeros((lines, 1), f32)
    ranks = []
    for n, piece in enumerate(pieces):
        here = upto[n * lines:(n + 1) * lines]
        ranks.append((here + (carry - 1.0)) * piece)
        carry = carry + here[:, STEP - 1:]
    ranks = jnp.concatenate(ranks, axis=1)
    for k in range(kinds):
        owners = owner[k]
        mine = hot[k * groups:(k + 1) * groups]
        rank = jnp.sum(ranks[k * groups:(k + 1) * groups], axis=0, keepdims=True).astype(i32)
        pos[half, k:k + 1, :] = owners * cap + rank
        wanted = row[k:k + 1, :]
        coarse = mine * (wanted >> 8).astype(f32)
        fine = mine * (wanted & 255).astype(f32)
        pair = jnp.concatenate([coarse, fine], axis=0).astype(bf16)
        listed = lax.dot_general(pair, one_hot(rank, cap), NT, preferred_element_type=f32)
        listed = (listed[:groups] * 256.0 + listed[groups:]).astype(i32)
        for o in range(groups):
            req_send[o, k:k + 1, :] = listed[o:o + 1]
    slots = lax.broadcasted_iota(i32, (1, edge_total), 1)
    for n, r in enumerate(RELATIONS):
        edges[half, n:n + 1, :] = jnp.where(
            slots < count[0, r], dst[r:r + 1, :] * sampled + src[r:r + 1, :], -1)

    pl.semaphore_wait(barrier, groups - 1 + shares - 1)
    asks = []
    for d in range(1, groups):
        to = lax.rem(g + d, groups)
        copy = pltpu.make_async_remote_copy(
            req_send.at[to], req_recv.at[g], req_ss.at[d], req_rs.at[d],
            device_id={"dp": to}, device_id_type=MESH)
        copy.start()
        asks.append(copy)
    hints = []
    for i in range(1, HALVES):
        to = lax.rem(half + i, HALVES) * side + q
        for n, ref in enumerate((pos, edges)):
            copy = pltpu.make_async_remote_copy(
                ref.at[half], ref.at[half], idx_ss.at[i, n], idx_rs.at[i, n],
                device_id={"dp": to}, device_id_type=MESH)
            copy.start()
            hints.append(copy)

    load_features.wait()
    for k in range(kinds):
        for h in range(high):
            tab[k, h * feat:(h + 1) * feat, :] = features[k, :, h * low:(h + 1) * low]

    def build(i, lo_r, hi_r):
        block = lax.rem(half + i, HALVES)

        def one(r, _):
            packed = edges[block, pl.ds(r, 1), :]
            live = packed >= 0
            source = packed & (sampled - 1)
            left = one_hot(jnp.where(live, source & (low - 1), -1), low)
            column = (source >> log2(low)) * SEEDS + (packed >> log2(sampled))
            right = one_hot(jnp.where(live, column, -1), s_high * SEEDS)
            counts = lax.dot_general(left, right, NT, preferred_element_type=f32)
            for h in range(s_high):
                adj[i, r, h * low:(h + 1) * low, :] = counts[:, h * SEEDS:(h + 1) * SEEDS].astype(bf16)
            total = jnp.sum(counts, axis=0, keepdims=True)
            seen = total[:, :SEEDS]
            for h in range(1, s_high):
                seen = seen + total[:, h * SEEDS:(h + 1) * SEEDS]
            deg[i, r] = jnp.broadcast_to(jnp.maximum(seen, 1.0), (8, SEEDS))
            return 0

        lax.fori_loop(core * share + lo_r, core * share + hi_r, one, 0)

    def share_block(i):
        built = pl.ds(core * share, share)
        copies = []
        for n, ref in enumerate((adj, deg)):
            copies.append(pltpu.make_async_remote_copy(
                ref.at[i, built], ref.at[i, built], adj_ss.at[i, n], adj_rs.at[i, n],
                device_id={"mp": m - core + lax.rem(core + 1, CORES)}, device_id_type=MESH))
            copies[-1].start()
        return copies

    build(0, 0, 1)
    req_recv[g] = req_send[g]
    for copy in asks:
        copy.wait()

    def pick(k, block):
        wanted = req_recv[block, k:k + 1, :]
        found = jnp.dot(tab[k], one_hot(wanted & (low - 1), low), preferred_element_type=f32)
        bank = wanted >> log2(low)
        chosen = jnp.zeros((feat, cap), f32)
        for h in range(high):
            chosen = jnp.where(bank == h, found[h * feat:(h + 1) * feat], chosen)
        return chosen.astype(bf16)

    def row_copy(k, d, j):
        return pltpu.make_async_remote_copy(
            send.at[k, d, j], recv.at[k, j, q], row_ss.at[k, d, j], row_rs.at[k, d, j],
            device_id={"dp": half * side + lax.rem(q + d, side)}, device_id_type=MESH)

    for k in range(kinds):
        def serve(n, _, k=k):
            d, j = 1 + lax.rem(n, side - 1), lax.rem(half + 1 + n // (side - 1), HALVES)
            send[k, d, j] = pick(k, j * side + lax.rem(q + d, side))
            row_copy(k, d, j).start()
            return 0

        lax.fori_loop(0, (side - 1) * HALVES, serve, 0)
    for k in range(kinds):
        def keep(j, _, k=k):
            recv[k, j, q] = pick(k, j * side + q)
            return 0

        lax.fori_loop(0, HALVES, keep, 0)

    build(0, 1, share)
    shared = share_block(0)
    for copy in hints:
        copy.wait()
    for i in range(1, HALVES):
        build(i, 0, share)
        shared += share_block(i)
    for copy in shared:
        copy.wait()

    replies = [[] for _ in range(kinds)]
    sums = [None] * kinds

    def finish(k):
        for copy in replies[k]:
            copy.wait()
        for n, matrix in enumerate(SLOTS[k]):
            message = part[STARTS[k] + n]
            for i in range(1, HALVES):
                message = message + part_recv[i, STARTS[k] + n].astype(f32)
            term = lax.dot_general(message.astype(bf16), weights[matrix], TN, preferred_element_type=f32)
            t = MATRIX_TARGET[matrix]
            sums[t] = term if sums[t] is None else sums[t] + term

    for k in range(kinds):
        start, size = STARTS[k], len(SLOTS[k])
        first = start - k
        for i in reversed(range(HALVES)):
            block = lax.rem(half + i, HALVES)

            def landed(n, _, k=k, block=block):
                row_copy(k, 1 + n, block).wait()
                return 0

            lax.fori_loop(0, side - 1, landed, 0)
            stack = recv[k, block].reshape(side * feat, cap)
            gathered = []
            for h in range(s_high):
                where = pos[block, k:k + 1, h * low:(h + 1) * low]
                found = jnp.dot(stack, one_hot(where & (cap - 1), cap), preferred_element_type=f32)
                holder = (where >> log2(cap)) - half * side
                chosen = jnp.zeros((feat, low), f32)
                for o in range(side):
                    chosen = jnp.where(holder == o, found[o * feat:(o + 1) * feat], chosen)
                gathered.append(chosen.astype(bf16))
            gathered = jnp.concatenate(gathered, axis=1)
            counts = jnp.concatenate([adj[i, first + n] for n in range(size - 1)], axis=1)
            summed = jnp.dot(gathered, counts, preferred_element_type=f32)
            values = [summed[:, n * SEEDS:(n + 1) * SEEDS] / deg[i, first + n][:1] for n in range(size - 1)]
            values.append(gathered[:, :SEEDS].astype(f32))
            for n, value in enumerate(values):
                if i == 0:
                    part[start + n] = value
                else:
                    part_send[i, start + n] = value.astype(bf16)
            if i > 0:
                copy = pltpu.make_async_remote_copy(
                    part_send.at[i, pl.ds(start, size)], part_recv.at[i, pl.ds(start, size)],
                    part_ss.at[i, k], part_rs.at[i, k],
                    device_id={"dp": block * side + q}, device_id_type=MESH)
                copy.start()
                replies[k].append(copy)
        if k == 0:
            load_weights.wait()
        else:
            finish(k - 1)
    finish(kinds - 1)
    width = typed.shape[3]
    for t in range(kinds):
        for p in range(shares):
            piece = sums[t][:, p * width:(p + 1) * width]
            typed[p, t] = piece
            typed_send[p, t] = piece.astype(bf16)
    last = []
    for d in range(1, shares):
        to = lax.rem(m + d, shares)
        copy = pltpu.make_async_remote_copy(
            typed_send.at[to], typed_recv.at[d], typed_ss.at[d], typed_rs.at[d],
            device_id={"mp": to}, device_id_type=MESH)
        copy.start()
        last.append(copy)
    for copy in last:
        copy.wait()
    for t in range(kinds):
        total = typed[m, t]
        for d in range(1, shares):
            total = total + typed_recv[d, t].astype(f32)
        out[t] = jnp.maximum(total, 0.0).T.astype(bf16)


def per_device(features, weights, sample_owner, sample_row, edge_src, edge_dst, edge_count):
    groups, shares = lax.axis_size("dp"), lax.axis_size("mp")
    kinds, feat, rows = features.shape
    sampled, edge_total = sample_row.shape[1], edge_src.shape[1]
    cap = 2 * sampled // groups
    low = min(512, rows, sampled)
    side = groups // HALVES
    width = weights.shape[2] // shares
    bf16, f32, i32 = jnp.bfloat16, jnp.float32, jnp.int32
    vmem = pl.BlockSpec(memory_space=pltpu.VMEM)
    any_space = pl.BlockSpec(memory_space=pl.ANY)
    dma = pltpu.SemaphoreType.DMA
    return pl.pallas_call(
        functools.partial(kernel, groups, shares),
        out_shape=jax.ShapeDtypeStruct((kinds, width, SEEDS), bf16),
        in_specs=[any_space] * 2 + [vmem] * 4 + [pl.BlockSpec(memory_space=pltpu.SMEM)],
        out_specs=vmem,
        scratch_shapes=[
            pltpu.VMEM(features.shape, bf16),
            pltpu.VMEM(weights.shape, bf16),
            dma((2,)),
            pltpu.VMEM((STEP, max(sampled, edge_total)), bf16),
            pltpu.VMEM((kinds, rows // low * feat, low), bf16),
            pltpu.VMEM((groups, kinds, cap), i32),
            pltpu.VMEM((groups, kinds, cap), i32),
            pltpu.VMEM((HALVES, kinds, sampled), i32),
            pltpu.VMEM((HALVES, RELS, edge_total), i32),
            pltpu.VMEM((kinds, side, HALVES, feat, cap), bf16),
            pltpu.VMEM((kinds, HALVES, side, feat, cap), bf16),
            pltpu.VMEM((HALVES, RELS, sampled, SEEDS), bf16),
            pltpu.VMEM((HALVES, RELS, 8, SEEDS), f32),
            pltpu.VMEM((MATS, feat, SEEDS), f32),
            pltpu.VMEM((HALVES, MATS, feat, SEEDS), bf16),
            pltpu.VMEM((HALVES, MATS, feat, SEEDS), bf16),
            pltpu.VMEM((shares, kinds, SEEDS, width), f32),
            pltpu.VMEM((shares, kinds, SEEDS, width), bf16),
            pltpu.VMEM((shares, kinds, SEEDS, width), bf16),
            dma((groups,)), dma((groups,)),
            dma((HALVES, 2)), dma((HALVES, 2)),
            dma((kinds, side, HALVES)), dma((kinds, side, HALVES)),
            dma((HALVES, kinds)), dma((HALVES, kinds)),
            dma((shares,)), dma((shares,)),
            dma((HALVES, 2)), dma((HALVES, 2)),
        ],
        compiler_params=pltpu.CompilerParams(
            collective_id=0, has_side_effects=True, vmem_limit_bytes=56 * 1024 * 1024),
    )(features, weights, sample_owner.transpose(0, 2, 1), sample_row, edge_src, edge_dst, edge_count.T)


def solution(mesh):
    return jax.shard_map(
        per_device,
        mesh=mesh,
        in_specs=(
            P(None, "mp", "dp"),
            P(None, "mp", None),
            P(None, "dp", None),
            P(None, "dp"),
            P(None, "dp"),
            P(None, "dp"),
            P(None, "dp"),
        ),
        out_specs=P(None, "mp", "dp"),
        check_vma=False,
    )
```

profile of v0, /device:TPU:0, one launch (start us, length us, event | category | flops | bytes accessed | tf_op | source)
XLA Modules:
  0.0 64.9 jit_solution(1590031040909671249)
XLA Ops:
  0.0 63.3 %shard_map.73 = bf16[3,128,128]{2,1,0:T(8,128)(2,1)} custom-call(bf16[3,128,2048]{2,1,0:T(8,128)(2,1)} %features_in.1, bf16[11,128,512]{2,1,0:T(8,128)(2,1)} %weights_in.1, s32[3,1,2048]{2,1,0:T(1,128)} %bitcast.2, s32[3,2048]{1,0:T(4,128)} %row.1, s32[8,2048]{1,0:T(8,128)} %src.1, s32[8,2048]{1,0:T(8,128)} %dst.1, s32[1,8]{1,0:T(1,128)} %bitcast.3), custom_call_target="tpu_custom_call" | custom-call | tf_op jit(solution)/shard_map/pallas_call | solution.py:301
  63.3 1.5 %copy.9 = bf16[3,128,128]{2,1,0:T(8,128)(2,1)} copy(bf16[3,128,128]{2,1,0:T(8,128)(2,1)} %shard_map.73) | data formatting | bytes 196608
where the time goes:
time: 65.4 us; the launch traced here: 64.9 us
  Pallas kernels  63.3 us (97%)
  local copies, waits for them, and re-layouts  1.54 us (2%)
    pallas_call x1, Pallas kernels, per_device(): pl.pallas_call(functools.partial(kernel, groups, shares), out_shape=jax.S...  63.3 us
    unnamed x1, local copies, waits for them, and re-layouts  1.54 us

commit v1 on v0

v1 whole, which is shorter than its diff:
```python
import functools

import jax
import jax.numpy as jnp
from jax import lax
from jax.experimental import pallas as pl
from jax.experimental.pallas import tpu as pltpu
from jax.sharding import PartitionSpec as P

SEEDS = 128
RELATION_SOURCE = (0, 1, 0, 1, 2, 0, 2, 1)
MATRIX_TARGET = (1, 0, 0, 2, 1, 2, 0, 1, 0, 1, 2)
RELS = len(RELATION_SOURCE)
KINDS = 3
MATS = RELS + KINDS
SLOTS = tuple(
    tuple([r for r in range(RELS) if RELATION_SOURCE[r] == k] + [RELS + k]) for k in range(KINDS)
)
ORDER = tuple(m for group in SLOTS for m in group)
STARTS = tuple(sum(len(group) for group in SLOTS[:k]) for k in range(KINDS))
PLACE = tuple(ORDER.index(m) for m in range(MATS))
CORES = 2
SHARE = RELS // CORES
STEP = 256
LANES = 128
MESH = pl.DeviceIdType.MESH
NT = (((1,), (1,)), ((), ()))


def log2(n):
    return n.bit_length() - 1


def kernel(groups, shares, features_in, weights_in, owner, row, src, dst, count, out,
           feats, weights, iota, req_send, req_recv, info_send, info_recv, table,
           lidx, ridx, picked, adj, message, hold, xsend, xrecv, zsend, zrecv,
           in_sem, fx_ss, fx_rs, req_ss, req_rs, info_ss, info_rs, x_ss, x_rs, z_ss, z_rs):
    kinds, _, feat, rows = feats.shape
    both = CORES * feat
    sampled = row.shape[1]
    edge_total = src.shape[1]
    cap = req_send.shape[2] - SEEDS
    low = min(512, rows)
    high = rows // low
    lo_n = min(STEP, cap)
    hi_n = cap // lo_n
    items = groups // CORES
    planes = shares // CORES
    half = hold.shape[3]
    quarter = half // CORES
    g = lax.axis_index("dp")
    m = lax.axis_index("mp")
    core = lax.rem(m, CORES)
    plane = m // CORES
    f32, bf16, i32 = jnp.float32, jnp.bfloat16, jnp.int32
    one, zero = jnp.ones((), bf16), jnp.zeros((), bf16)

    def at(group, mp):
        return {"dp": group, "mp": mp}

    def remote(source, target, ss, rs, group, mp):
        return pltpu.make_async_remote_copy(source, target, ss, rs, device_id=at(group, mp), device_id_type=MESH)

    def hits(index, size):
        n = index.shape[1]
        return jnp.where(iota[:size, :n] == index.astype(f32).astype(bf16), one, zero)

    mate = m - core + lax.rem(core + 1, CORES)
    loads, swaps = [], []
    for k in range(kinds):
        loads.append(pltpu.make_async_copy(features_in.at[k], feats.at[k, core], in_sem.at[k]))
        swaps.append(remote(features_in.at[k], feats.at[k, core], fx_ss.at[k], fx_rs.at[k], g, mate))
    loads.append(pltpu.make_async_copy(weights_in, weights.at[core], in_sem.at[kinds]))
    swaps.append(remote(weights_in, weights.at[core], fx_ss.at[kinds], fx_rs.at[kinds], g, mate))
    for copy in loads:
        copy.start()

    barrier = pltpu.get_barrier_semaphore()
    pl.semaphore_signal(barrier, inc=1, device_id=at(g, mate), device_id_type=MESH)
    for d in range(1, groups):
        for c in range(CORES):
            pl.semaphore_signal(barrier, inc=1, device_id=at(g ^ d, plane * CORES + c), device_id_type=MESH)
    for e in range(1, planes):
        pl.semaphore_signal(
            barrier, inc=1, device_id=at(g, lax.rem(plane + e, planes) * CORES + core), device_id_type=MESH)

    iota[...] = lax.broadcasted_iota(i32, iota.shape, 0).astype(f32).astype(bf16)
    tri = (lax.broadcasted_iota(i32, (STEP, STEP), 0) <= lax.broadcasted_iota(i32, (STEP, STEP), 1))
    tri = jnp.where(tri, 1.0, 0.0).astype(bf16)
    hot = jnp.concatenate([
        jnp.where(lax.broadcasted_iota(i32, (groups, sampled), 0) == owner[k], 1.0, 0.0)
        for k in range(kinds)], axis=0)
    lines = kinds * groups
    pieces = [hot[:, base:base + STEP] for base in range(0, sampled, STEP)]
    upto = jnp.dot(jnp.concatenate(pieces, axis=0).astype(bf16), tri, preferred_element_type=f32)
    carry = jnp.zeros((lines, 1), f32)
    ranks = []
    for n, piece in enumerate(pieces):
        here = upto[n * lines:(n + 1) * lines]
        ranks.append((here + (carry - 1.0)) * piece)
        carry = carry + here[:, STEP - 1:]
    ranks = jnp.concatenate(ranks, axis=1)

    pl.semaphore_wait(barrier, CORES * (groups - 1) + planes)
    for copy in swaps:
        copy.start()

    blocks = sampled // LANES
    parts = cap // LANES
    for k in range(kinds):
        mine = hot[k * groups:(k + 1) * groups]
        rank = jnp.sum(ranks[k * groups:(k + 1) * groups], axis=0, keepdims=True).astype(i32)
        place = owner[k] * cap + rank
        coarse = (place >> 8).astype(f32)
        fine = (place & 255).astype(f32)
        table[k] = jnp.concatenate(
            [part[:, b * LANES:(b + 1) * LANES] for part in (coarse, fine) for b in range(blocks)], axis=0).astype(bf16)
        wanted = row[k:k + 1, :]
        tall = mine * (wanted >> 8).astype(f32)
        wide = mine * (wanted & 255).astype(f32)
        bank = rank >> log2(LANES)
        stack = jnp.concatenate(
            [jnp.where(bank == h, part, 0.0) for part in (tall, wide) for h in range(parts)], axis=0).astype(bf16)
        listed = lax.dot_general(stack, hits(rank & (LANES - 1), LANES), NT, preferred_element_type=f32)
        listed = (listed[:parts * groups] * 256.0 + listed[parts * groups:]).astype(i32)
        seeds = jnp.where(mine[:, :SEEDS] > 0.0, rank[:, :SEEDS], -1)
        for o in range(groups):
            for h in range(parts):
                req_send[o, k:k + 1, h * LANES:(h + 1) * LANES] = listed[h * groups + o:h * groups + o + 1]
            req_send[o, k:k + 1, cap:] = seeds[o:o + 1]

    requests = []
    def order(i):
        return 0 if i == 0 else 1 if i == items - 1 else i + 1

    def request_copy(t):
        to = g ^ (CORES * t + core)
        return remote(req_send.at[to], req_recv.at[t], req_ss.at[t], req_rs.at[t], to, m)

    for i in range(items):
        t = order(i)
        if t == 0:
            @pl.when(core > 0)
            def _():
                request_copy(0).start()

            @pl.when(core == 0)
            def _():
                req_recv[0] = req_send[g]
        else:
            request_copy(t).start()

    slots = lax.broadcasted_iota(i32, (1, edge_total), 1)
    banks = lax.broadcasted_iota(i32, (blocks, edge_total), 0)
    ones8 = jnp.ones((8, LANES), bf16)
    for j in range(SHARE):
        r = core * SHARE + j
        kind = RELATION_SOURCE[j] + core * (RELATION_SOURCE[SHARE + j] - RELATION_SOURCE[j])
        wanted = src[pl.ds(r, 1), :]
        found = jnp.dot(table[kind], hits(wanted & (LANES - 1), LANES), preferred_element_type=f32)
        found = found[:blocks] * 256.0 + found[blocks:]
        found = jnp.where(banks == (wanted >> log2(LANES)), found, 0.0)
        place = jnp.sum(found, axis=0, keepdims=True).astype(i32)
        live = slots < count[0, r]
        ends = dst[pl.ds(r, 1), :]
        info_send[j:j + 1, :edge_total] = jnp.where(live, place * SEEDS + ends, -1)
        marks = hits(jnp.where(live, ends, -1), SEEDS)
        tally = marks[:, :LANES]
        for base in range(LANES, edge_total, LANES):
            tally = tally + marks[:, base:base + LANES]
        tally = lax.dot_general(ones8, tally, NT, preferred_element_type=f32)
        info_send[j:j + 1, edge_total:] = tally[:1].astype(i32)

    def info_copy(d):
        return remote(info_send, info_recv.at[d // CORES, core], info_ss.at[d], info_rs.at[d // CORES, core],
                      g ^ d, plane * CORES + d % CORES)

    for i in range(items):
        for c in reversed(range(CORES)):
            d = CORES * order(i) + c
            if d == 0:
                @pl.when(core > 0)
                def _():
                    info_copy(0).start()

                @pl.when(core == 0)
                def _():
                    info_recv[0, 0] = info_send[...]
            else:
                info_copy(d).start()

    def info_wait(t, c):
        remote(info_send, info_recv.at[t, c], info_ss.at[0], info_rs.at[t, c], g, mate).wait_recv()

    for copy in loads:
        copy.wait()
    for copy in swaps:
        copy.wait()

    def x_copy(i, e, t):
        to = lax.rem(plane + e, planes) * CORES + core
        return remote(xsend.at[i, e, t], xrecv.at[i, e, t], x_ss.at[i, e, t], x_rs.at[i, e, t], g, to)

    def z_copy(i, d, c, t):
        return remote(zsend.at[i, c, t], zrecv.at[d, t], z_ss.at[i, c, t], z_rs.at[d, t],
                      g ^ d, plane * CORES + c)

    def spot(i):
        return jnp.where(i == 0, 0, jnp.where(i == items - 1, 1, i + 1))

    def forward(i, t):
        d = CORES * spot(i) + core
        total = hold[i, t]
        for e in range(1, planes):
            x_copy(i, e, t).wait_recv()
            total = total + xrecv[i, e, t].astype(f32)
        total = total.astype(bf16)
        for c in range(CORES):
            zsend[i, c, t] = total[:, c * quarter:(c + 1) * quarter]
        for c in range(1, CORES):
            z_copy(i, d, c, t).start()

        @pl.when(d > 0)
        def _():
            z_copy(i, d, 0, t).start()

        @pl.when(d == 0)
        def _():
            zrecv[0, t] = total[:, :quarter]

    def build(place, ref_l, ref_r, n, width):
        left = hits(ref_l[pl.ds(n, 1), :width], lo_n) if width <= STEP else jnp.concatenate(
            [hits(ref_l[pl.ds(n, 1), base:base + STEP], lo_n) for base in range(0, width, STEP)], axis=1)
        right = hits(ref_r[pl.ds(n, 1), :width], hi_n * SEEDS) if width <= STEP else jnp.concatenate(
            [hits(ref_r[pl.ds(n, 1), base:base + STEP], hi_n * SEEDS) for base in range(0, width, STEP)], axis=1)
        counts = lax.dot_general(right, left, NT, preferred_element_type=f32).astype(bf16)
        for h in range(hi_n):
            adj[place, :, h * lo_n:(h + 1) * lo_n] = counts[h * SEEDS:(h + 1) * SEEDS]

    def item(i, _):
        t = spot(i)
        d = CORES * t + core

        @pl.when(d > 0)
        def _():
            request_copy(t).wait_recv()
            info_wait(t, 0)

        info_wait(t, 1)
        for k in range(kinds):
            wanted = req_recv[t, k:k + 1, :cap]
            table_k = feats[k].reshape(both, rows)
            table_k = jnp.concatenate([table_k[:, h * low:(h + 1) * low] for h in range(high)], axis=0)
            fine = wanted & (low - 1)
            choice = jnp.concatenate(
                [hits(jnp.where((fine >= base) & (fine < base + STEP), fine - base, -1), STEP)
                 for base in range(0, low, STEP)], axis=0)
            found = jnp.dot(table_k, choice, preferred_element_type=f32)
            bank = wanted >> log2(low)
            chosen = found[:both]
            for h in range(1, high):
                chosen = jnp.where(bank == h, found[h * both:(h + 1) * both], chosen)
            picked[k] = chosen.astype(bf16)

        for c in range(CORES):
            packed = info_recv[t, c, :, :edge_total] - g * (cap * SEEDS)
            ok = (packed >= 0) & (packed < cap * SEEDS)
            slot = packed >> log2(SEEDS)
            lidx[c * SHARE:(c + 1) * SHARE, :] = (slot & (lo_n - 1)).astype(f32)
            ridx[c * SHARE:(c + 1) * SHARE, :] = jnp.where(
                ok, (slot >> log2(lo_n)) * SEEDS + (packed & (SEEDS - 1)), -1).astype(f32)
        slot = req_recv[t, :, cap:]
        lidx[RELS:RELS + kinds, :SEEDS] = (slot & (lo_n - 1)).astype(f32)
        ridx[RELS:RELS + kinds, :SEEDS] = jnp.where(
            slot >= 0, (slot >> log2(lo_n)) * SEEDS + lax.broadcasted_iota(i32, slot.shape, 1), -1).astype(f32)

        def relation(r, _):
            build(r, lidx, ridx, r, edge_total)
            return 0

        lax.fori_loop(0, RELS, relation, 0)
        for k in range(kinds):
            build(RELS + k, lidx, ridx, RELS + k, SEEDS)

        @pl.when(i > 0)
        def _():
            for n in range(kinds):
                forward(i - 1, n)

        degree = jnp.concatenate([info_recv[t, c, :, edge_total:] for c in range(CORES)], axis=0)
        inverse = (1.0 / jnp.maximum(degree.astype(f32), 1.0)).T
        for k in range(kinds):
            group = SLOTS[k]
            counts = jnp.concatenate([adj[n] for n in group], axis=0)
            summed = lax.dot_general(counts, picked[k], NT, preferred_element_type=f32)
            for n, matrix in enumerate(group):
                value = summed[n * SEEDS:(n + 1) * SEEDS]
                if matrix < RELS:
                    value = value * inverse[:, matrix:matrix + 1]
                message[matrix] = value.astype(bf16)
        for n in range(kinds):
            group = [matrix for matrix in range(MATS) if MATRIX_TARGET[matrix] == n]
            left = jnp.concatenate([message[matrix] for matrix in group], axis=1)
            right = jnp.concatenate([weights[c, matrix] for matrix in group for c in range(CORES)], axis=0)
            typed = jnp.dot(left, right, preferred_element_type=f32)
            for p in range(planes):
                piece = typed[:, p * half:(p + 1) * half]

                @pl.when(plane == p)
                def _(piece=piece, n=n):
                    hold[i, n] = piece

                @pl.when(plane != p)
                def _(piece=piece, n=n, p=p):
                    xsend[i, lax.rem(p - plane + planes, planes), n] = piece.astype(bf16)
            for e in range(1, planes):
                x_copy(i, e, n).start()
        return 0

    lax.fori_loop(0, items, item, 0)
    for n in range(kinds):
        forward(items - 1, n)

    for n in range(kinds):
        total = jnp.zeros((SEEDS, quarter), f32)
        for i in range(items):
            for c in reversed(range(CORES)):
                d = CORES * order(i) + c
                if d == 0:
                    @pl.when(core > 0)
                    def _():
                        z_copy(0, 0, 0, n).wait_recv()
                else:
                    z_copy(0, d, 0, n).wait_recv()
                total = total + zrecv[d, n].astype(f32)
        out[n] = jnp.maximum(total, 0.0).T.astype(bf16)

    for t in range(items):
        if t == 0:
            @pl.when(core > 0)
            def _():
                request_copy(0).wait_send()
                info_copy(0).wait_send()
        else:
            request_copy(t).wait_send()
            info_copy(CORES * t).wait_send()
        for c in range(1, CORES):
            info_copy(CORES * t + c).wait_send()
        for n in range(kinds):
            for e in range(1, planes):
                x_copy(t, e, n).wait_send()
            d = CORES * spot(t) + core
            for c in range(1, CORES):
                z_copy(t, d, c, n).wait_send()

            @pl.when(d > 0)
            def _():
                z_copy(t, d, 0, n).wait_send()


def per_device(features, weights, sample_owner, sample_row, edge_src, edge_dst, edge_count):
    groups, shares = lax.axis_size("dp"), lax.axis_size("mp")
    kinds, feat, rows = features.shape
    sampled, edge_total = sample_row.shape[1], edge_src.shape[1]
    cap = 2 * sampled // groups
    items, planes = groups // CORES, shares // CORES
    width = weights.shape[2]
    half, quarter = width // planes, width // shares
    bf16, f32, i32 = jnp.bfloat16, jnp.float32, jnp.int32
    vmem = pl.BlockSpec(memory_space=pltpu.VMEM)
    any_space = pl.BlockSpec(memory_space=pl.ANY)
    dma = pltpu.SemaphoreType.DMA
    return pl.pallas_call(
        functools.partial(kernel, groups, shares),
        out_shape=jax.ShapeDtypeStruct((kinds, quarter, SEEDS), bf16),
        in_specs=[any_space] * 2 + [vmem] * 4 + [pl.BlockSpec(memory_space=pltpu.SMEM)],
        out_specs=vmem,
        scratch_shapes=[
            pltpu.VMEM((kinds, CORES, feat, rows), bf16),
            pltpu.VMEM((CORES, MATS, feat, width), bf16),
            pltpu.VMEM((STEP, max(sampled, edge_total)), bf16),
            pltpu.VMEM((groups, kinds, cap + SEEDS), i32),
            pltpu.VMEM((items, kinds, cap + SEEDS), i32),
            pltpu.VMEM((SHARE, edge_total + SEEDS), i32),
            pltpu.VMEM((items, CORES, SHARE, edge_total + SEEDS), i32),
            pltpu.VMEM((kinds, 2 * sampled // LANES, LANES), bf16),
            pltpu.VMEM((16, edge_total), f32),
            pltpu.VMEM((16, edge_total), f32),
            pltpu.VMEM((kinds, CORES * feat, cap), bf16),
            pltpu.VMEM((MATS, SEEDS, cap), bf16),
            pltpu.VMEM((MATS, SEEDS, CORES * feat), bf16),
            pltpu.VMEM((items, kinds, SEEDS, half), f32),
            pltpu.VMEM((items, planes, kinds, SEEDS, half), bf16),
            pltpu.VMEM((items, planes, kinds, SEEDS, half), bf16),
            pltpu.VMEM((items, CORES, kinds, SEEDS, quarter), bf16),
            pltpu.VMEM((groups, kinds, SEEDS, quarter), bf16),
            dma((kinds + 1,)), dma((kinds + 1,)), dma((kinds + 1,)),
            dma((items,)), dma((items,)),
            dma((groups,)), dma((items, CORES)),
            dma((items, planes, kinds)), dma((items, planes, kinds)),
            dma((items, CORES, kinds)), dma((groups, kinds)),
        ],
        compiler_params=pltpu.CompilerParams(
            collective_id=0, has_side_effects=True, vmem_limit_bytes=60 * 1024 * 1024),
    )(features, weights, sample_owner.transpose(0, 2, 1), sample_row, edge_src, edge_dst, edge_count.T)


def solution(mesh):
    return jax.shard_map(
        per_device,
        mesh=mesh,
        in_specs=(
            P(None, "mp", "dp"),
            P(None, "mp", None),
            P(None, "dp", None),
            P(None, "dp"),
            P(None, "dp"),
            P(None, "dp"),
            P(None, "dp"),
        ),
        out_specs=P(None, "mp", "dp"),
        check_vma=False,
    )
```

time: 65.4 us -> 56.1 us (0.86)
  Pallas kernels: 63.3 us -> 54.4 us
    pallas_call x1, Pallas kernels: 63.3 us -> 54.4 us  [per_device(): pl.pallas_call(functools.partial(kernel, groups, shares), out_shape=jax.S...]
where the time goes in v1:
time: 56.1 us; the launch traced here: 55.9 us
  Pallas kernels  54.4 us (97%)
  local copies, waits for them, and re-layouts  1.54 us (3%)
    pallas_call x1, Pallas kernels, per_device(): pl.pallas_call(functools.partial(kernel, groups, shares), out_shape=jax.S...  54.4 us
    unnamed x1, local copies, waits for them, and re-layouts  1.54 us

profile of v1, /device:TPU:0, one launch (start us, length us, event | category | flops | bytes accessed | tf_op | source)
XLA Modules:
  0.0 55.9 jit_solution(11385866048357334972)
XLA Ops:
  0.0 54.4 %shard_map.73 = bf16[3,128,128]{2,1,0:T(8,128)(2,1)} custom-call(bf16[3,128,2048]{2,1,0:T(8,128)(2,1)} %features_in.1, bf16[11,128,512]{2,1,0:T(8,128)(2,1)} %weights_in.1, s32[3,1,2048]{2,1,0:T(1,128)} %bitcast.2, s32[3,2048]{1,0:T(4,128)} %row.1, s32[8,2048]{1,0:T(8,128)} %src.1, s32[8,2048]{1,0:T(8,128)} %dst.1, s32[1,8]{1,0:T(1,128)} %bitcast.3), custom_call_target="tpu_custom_call" | custom-call | tf_op jit(solution)/shard_map/pallas_call | solution.py:373
  54.4 1.5 %copy.9 = bf16[3,128,128]{2,1,0:T(8,128)(2,1)} copy(bf16[3,128,128]{2,1,0:T(8,128)(2,1)} %shard_map.73) | data formatting | bytes 196608

commit v2 on v1

--- a/solution.py
+++ b/solution.py
@@ -20,6 +20,7 @@
 STARTS = tuple(sum(len(group) for group in SLOTS[:k]) for k in range(KINDS))
 PLACE = tuple(ORDER.index(m) for m in range(MATS))
 CORES = 2
+WAYS = 2
 SHARE = RELS // CORES
 STEP = 256
 LANES = 128
@@ -33,8 +34,8 @@
 
 def kernel(groups, shares, features_in, weights_in, owner, row, src, dst, count, out,
            feats, weights, iota, req_send, req_recv, info_send, info_recv, table,
-           lidx, ridx, picked, adj, message, hold, xsend, xrecv, zsend, zrecv,
-           in_sem, fx_ss, fx_rs, req_ss, req_rs, info_ss, info_rs, x_ss, x_rs, z_ss, z_rs):
+           lidx, ridx, picked, adj, xsend, xrecv, yrecv, zsend, zrecv,
+           in_sem, fx_ss, fx_rs, req_ss, req_rs, info_ss, info_rs, x_ss, x_rs, y_ss, y_rs, z_ss, z_rs, own_ss, own_rs):
     kinds, _, feat, rows = feats.shape
     both = CORES * feat
     sampled = row.shape[1]
@@ -46,8 +47,9 @@
     hi_n = cap // lo_n
     items = groups // CORES
     planes = shares // CORES
-    half = hold.shape[3]
-    quarter = half // CORES
+    quarter = xsend.shape[6]
+    span = SEEDS // WAYS
+    half = CORES * quarter
     g = lax.axis_index("dp")
     m = lax.axis_index("mp")
     core = lax.rem(m, CORES)
@@ -129,9 +131,8 @@
                 req_send[o, k:k + 1, h * LANES:(h + 1) * LANES] = listed[h * groups + o:h * groups + o + 1]
             req_send[o, k:k + 1, cap:] = seeds[o:o + 1]
 
-    requests = []
     def order(i):
-        return 0 if i == 0 else 1 if i == items - 1 else i + 1
+        return i + 2 if i < items - 2 else items - 1 - i
 
     def request_copy(t):
         to = g ^ (CORES * t + core)
@@ -192,41 +193,65 @@
     def info_wait(t, c):
         remote(info_send, info_recv.at[t, c], info_ss.at[0], info_rs.at[t, c], g, mate).wait_recv()
 
-    for copy in loads:
-        copy.wait()
-    for copy in swaps:
-        copy.wait()
-
-    def x_copy(i, e, t):
+    def x_copy(i, w, e, t):
         to = lax.rem(plane + e, planes) * CORES + core
-        return remote(xsend.at[i, e, t], xrecv.at[i, e, t], x_ss.at[i, e, t], x_rs.at[i, e, t], g, to)
-
-    def z_copy(i, d, c, t):
-        return remote(zsend.at[i, c, t], zrecv.at[d, t], z_ss.at[i, c, t], z_rs.at[d, t],
+        return remote(xsend.at[i, t, w, e], xrecv.at[i, t, w, e], x_ss.at[i, t, w, e], x_rs.at[i, t, w, e], g, to)
+
+    def y_copy(i, t):
+        return remote(xsend.at[i, t, 1], yrecv.at[i, t], y_ss.at[i, t], y_rs.at[i, t], g ^ 1, plane * CORES)
+
+    def z_copy(i, d, c, t, w):
+        return remote(zsend.at[i, t, w, c], zrecv.at[d, t, w], z_ss.at[i, t, w, c], z_rs.at[d, t, w],
                       g ^ d, plane * CORES + c)
 
+    def far(e, d):
+        return d if e == 0 else groups + (e - 1) * CORES + d
+
+    def own_copy(e, c, t, d):
+        return remote(xsend.at[items - 1, t, :, e, c], zrecv.at[far(e, d), t], own_ss.at[t, e, c], own_rs.at[t, e, d],
+                      g ^ d, lax.rem(plane + e, planes) * CORES + c)
+
     def spot(i):
-        return jnp.where(i == 0, 0, jnp.where(i == items - 1, 1, i + 1))
-
-    def forward(i, t):
+        return jnp.where(i < items - 2, i + 2, items - 1 - i)
+
+    def merge(i):
+        for n in range(kinds):
+            y_copy(i, n).wait_recv()
+            for e in range(planes):
+                for c in range(CORES):
+                    total = xsend[i, n, 1, e, c].astype(f32) + yrecv[i, n, e, c].astype(f32)
+                    xsend[i, n, 1, e, c] = total.astype(bf16)
+            for e in range(1, planes):
+                x_copy(i, 1, e, n).start()
+
+    def deliver(i, w):
         d = CORES * spot(i) + core
-        total = hold[i, t]
-        for e in range(1, planes):
-            x_copy(i, e, t).wait_recv()
-            total = total + xrecv[i, e, t].astype(f32)
-        total = total.astype(bf16)
-        for c in range(CORES):
-            zsend[i, c, t] = total[:, c * quarter:(c + 1) * quarter]
-        for c in range(1, CORES):
-            z_copy(i, d, c, t).start()
-
-        @pl.when(d > 0)
-        def _():
-            z_copy(i, d, 0, t).start()
-
-        @pl.when(d == 0)
-        def _():
-            zrecv[0, t] = total[:, :quarter]
+        for n in range(kinds):
+            for e in range(1, planes):
+                x_copy(i, w, e, n).wait_recv()
+            for c in range(CORES):
+                total = xsend[i, n, w, 0, c].astype(f32)
+                for e in range(1, planes):
+                    total = total + xrecv[i, n, w, e, c].astype(f32)
+                zsend[i, n, w, c] = total.astype(bf16)
+            for c in range(CORES):
+                z_copy(i, d, c, n, w).start()
+
+    def pick(t, where):
+        for k in range(kinds):
+            wanted = req_recv[t, k:k + 1, :cap]
+            bank = wanted >> log2(low)
+            fine = wanted & (low - 1)
+            choice = jnp.concatenate(
+                [hits(jnp.where((fine >= base) & (fine < base + STEP), fine - base, -1), STEP)
+                 for base in range(0, low, STEP)], axis=0)
+            table_k = feats[k].reshape(both, rows)
+            table_k = jnp.concatenate([table_k[:, h * low:(h + 1) * low] for h in range(high)], axis=0)
+            found = jnp.dot(table_k, choice, preferred_element_type=f32)
+            chosen = found[:both]
+            for h in range(1, high):
+                chosen = jnp.where(bank == h, found[h * both:(h + 1) * both], chosen)
+            picked[where, k] = chosen.astype(bf16).T
 
     def build(place, ref_l, ref_r, n, width):
         left = hits(ref_l[pl.ds(n, 1), :width], lo_n) if width <= STEP else jnp.concatenate(
@@ -237,31 +262,22 @@
         for h in range(hi_n):
             adj[place, :, h * lo_n:(h + 1) * lo_n] = counts[h * SEEDS:(h + 1) * SEEDS]
 
-    def item(i, _):
-        t = spot(i)
-        d = CORES * t + core
-
-        @pl.when(d > 0)
-        def _():
+    def item(i, first, last):
+        t = order(i) if first or last else spot(i)
+        where = 1 if last else 0
+        if not last:
             request_copy(t).wait_recv()
+            pick(t, 0)
+        if last:
+            @pl.when(core > 0)
+            def _():
+                info_wait(t, 0)
+        else:
             info_wait(t, 0)
-
         info_wait(t, 1)
-        for k in range(kinds):
-            wanted = req_recv[t, k:k + 1, :cap]
-            table_k = feats[k].reshape(both, rows)
-            table_k = jnp.concatenate([table_k[:, h * low:(h + 1) * low] for h in range(high)], axis=0)
-            fine = wanted & (low - 1)
-            choice = jnp.concatenate(
-                [hits(jnp.where((fine >= base) & (fine < base + STEP), fine - base, -1), STEP)
-                 for base in range(0, low, STEP)], axis=0)
-            found = jnp.dot(table_k, choice, preferred_element_type=f32)
-            bank = wanted >> log2(low)
-            chosen = found[:both]
-            for h in range(1, high):
-                chosen = jnp.where(bank == h, found[h * both:(h + 1) * both], chosen)
-            picked[k] = chosen.astype(bf16)
-
+        if first:
+            loads[kinds].wait()
+            swaps[kinds].wait()
         for c in range(CORES):
             packed = info_recv[t, c, :, :edge_total] - g * (cap * SEEDS)
             ok = (packed >= 0) & (packed < cap * SEEDS)
@@ -273,66 +289,117 @@
         lidx[RELS:RELS + kinds, :SEEDS] = (slot & (lo_n - 1)).astype(f32)
         ridx[RELS:RELS + kinds, :SEEDS] = jnp.where(
             slot >= 0, (slot >> log2(lo_n)) * SEEDS + lax.broadcasted_iota(i32, slot.shape, 1), -1).astype(f32)
-
-        def relation(r, _):
-            build(r, lidx, ridx, r, edge_total)
-            return 0
-
-        lax.fori_loop(0, RELS, relation, 0)
-        for k in range(kinds):
-            build(RELS + k, lidx, ridx, RELS + k, SEEDS)
-
-        @pl.when(i > 0)
-        def _():
-            for n in range(kinds):
-                forward(i - 1, n)
-
         degree = jnp.concatenate([info_recv[t, c, :, edge_total:] for c in range(CORES)], axis=0)
         inverse = (1.0 / jnp.maximum(degree.astype(f32), 1.0)).T
-        for k in range(kinds):
-            group = SLOTS[k]
-            counts = jnp.concatenate([adj[n] for n in group], axis=0)
-            summed = lax.dot_general(counts, picked[k], NT, preferred_element_type=f32)
-            for n, matrix in enumerate(group):
-                value = summed[n * SEEDS:(n + 1) * SEEDS]
+        groups_of = [[matrix for matrix in range(MATS) if MATRIX_TARGET[matrix] == n] for n in range(kinds)]
+
+        def make(matrix):
+            build(matrix, lidx, ridx, matrix, edge_total if matrix < RELS else SEEDS)
+
+        def gather(n):
+            values = []
+            for matrix in groups_of[n]:
+                kind = RELATION_SOURCE[matrix] if matrix < RELS else matrix - RELS
+                value = jnp.dot(adj[matrix], picked[where, kind], preferred_element_type=f32)
                 if matrix < RELS:
                     value = value * inverse[:, matrix:matrix + 1]
-                message[matrix] = value.astype(bf16)
-        for n in range(kinds):
-            group = [matrix for matrix in range(MATS) if MATRIX_TARGET[matrix] == n]
-            left = jnp.concatenate([message[matrix] for matrix in group], axis=1)
-            right = jnp.concatenate([weights[c, matrix] for matrix in group for c in range(CORES)], axis=0)
-            typed = jnp.dot(left, right, preferred_element_type=f32)
+                values.append(value.astype(bf16))
+            return jnp.concatenate(values, axis=1)
+
+        def emit(n, left):
+            right = jnp.concatenate([weights[c, matrix] for matrix in groups_of[n] for c in range(CORES)], axis=0)
+            typed = jnp.dot(left, right, preferred_element_type=f32).astype(bf16)
             for p in range(planes):
-                piece = typed[:, p * half:(p + 1) * half]
-
-                @pl.when(plane == p)
-                def _(piece=piece, n=n):
-                    hold[i, n] = piece
-
-                @pl.when(plane != p)
-                def _(piece=piece, n=n, p=p):
-                    xsend[i, lax.rem(p - plane + planes, planes), n] = piece.astype(bf16)
-            for e in range(1, planes):
-                x_copy(i, e, n).start()
+                for w in range(WAYS):
+                    for c in range(CORES):
+                        xsend[i, n, w, lax.rem(p - plane + planes, planes), c] = typed[
+                            w * span:(w + 1) * span, p * half + c * quarter:p * half + (c + 1) * quarter]
+            if last:
+                for e in reversed(range(planes)):
+                    for c in range(CORES):
+                        if e or c:
+                            own_copy(e, c, n, core).start()
+
+                @pl.when(core > 0)
+                def _():
+                    own_copy(0, 0, n, core).start()
+
+                @pl.when(core == 0)
+                def _():
+                    for w in range(WAYS):
+                        zrecv[0, n, w] = xsend[i, n, w, 0, 0]
+            else:
+                for e in range(1, planes):
+                    x_copy(i, 0, e, n).start()
+
+                @pl.when(core > 0)
+                def _():
+                    y_copy(i, n).start()
+
+        for matrix in groups_of[0] + groups_of[1][:1]:
+            make(matrix)
+        left = gather(0)
+        make(groups_of[1][1])
+        emit(0, left)
+        if not first:
+            @pl.when((i >= 2) & (core == 0))
+            def _():
+                deliver(i - 2, 1)
+
+            @pl.when(core == 0)
+            def _():
+                merge(i - 1)
+
+            deliver(i - 1, 0)
+        for matrix in groups_of[1][2:] + groups_of[2][:1]:
+            make(matrix)
+        left = gather(1)
+        for matrix in groups_of[2][1:]:
+            make(matrix)
+        emit(1, left)
+        emit(2, gather(2))
+        if last:
+            @pl.when(core == 0)
+            def _():
+                deliver(i - 1, 1)
+
+    def rest(i, _):
+        item(i, False, False)
         return 0
 
-    lax.fori_loop(0, items, item, 0)
+    for k in range(kinds):
+        loads[k].wait()
+        swaps[k].wait()
+
+    @pl.when(core > 0)
+    def _():
+        request_copy(0).wait_recv()
+    pick(0, 1)
+    item(0, True, False)
+    lax.fori_loop(1, items - 1, rest, 0)
+    item(items - 1, False, True)
+
     for n in range(kinds):
-        forward(items - 1, n)
-
-    for n in range(kinds):
-        total = jnp.zeros((SEEDS, quarter), f32)
-        for i in range(items):
-            for c in reversed(range(CORES)):
-                d = CORES * order(i) + c
-                if d == 0:
+        halves = []
+        for w in range(WAYS):
+            total = jnp.zeros((span, quarter), f32)
+            for i in range(items - 1):
+                for c in range(CORES if w == 0 else 1):
+                    d = CORES * order(i) + c
+                    z_copy(0, d, 0, n, w).wait_recv()
+                    total = total + zrecv[d, n, w].astype(f32)
+            halves.append(total)
+        for e in range(planes):
+            for d in range(CORES):
+                if e or d:
+                    own_copy(e, 0, n, d).wait_recv()
+                else:
                     @pl.when(core > 0)
                     def _():
-                        z_copy(0, 0, 0, n).wait_recv()
-                else:
-                    z_copy(0, d, 0, n).wait_recv()
-                total = total + zrecv[d, n].astype(f32)
+                        own_copy(0, 0, n, 0).wait_recv()
+                for w in range(WAYS):
+                    halves[w] = halves[w] + zrecv[far(e, d), n, w].astype(f32)
+        total = jnp.concatenate(halves, axis=0)
         out[n] = jnp.maximum(total, 0.0).T.astype(bf16)
 
     for t in range(items):
@@ -346,16 +413,35 @@
             info_copy(CORES * t).wait_send()
         for c in range(1, CORES):
             info_copy(CORES * t + c).wait_send()
+    for i in range(items - 1):
+        d = CORES * order(i) + core
         for n in range(kinds):
             for e in range(1, planes):
-                x_copy(t, e, n).wait_send()
-            d = CORES * spot(t) + core
-            for c in range(1, CORES):
-                z_copy(t, d, c, n).wait_send()
-
-            @pl.when(d > 0)
-            def _():
-                z_copy(t, d, 0, n).wait_send()
+                x_copy(i, 0, e, n).wait_send()
+            for c in range(CORES):
+                z_copy(i, d, c, n, 0).wait_send()
+
+        @pl.when(core == 0)
+        def _():
+            for n in range(kinds):
+                for e in range(1, planes):
+                    x_copy(i, 1, e, n).wait_send()
+                for c in range(CORES):
+                    z_copy(i, d, c, n, 1).wait_send()
+
+        @pl.when(core > 0)
+        def _():
+            for n in range(kinds):
+                y_copy(i, n).wait_send()
+    for n in range(kinds):
+        for e in range(planes):
+            for c in range(CORES):
+                if e or c:
+                    own_copy(e, c, n, core).wait_send()
+
+        @pl.when(core > 0)
+        def _():
+            own_copy(0, 0, n, core).wait_send()
 
 
 def per_device(features, weights, sample_owner, sample_row, edge_src, edge_dst, edge_count):
@@ -365,7 +451,7 @@
     cap = 2 * sampled // groups
     items, planes = groups // CORES, shares // CORES
     width = weights.shape[2]
-    half, quarter = width // planes, width // shares
+    quarter = width // shares
     bf16, f32, i32 = jnp.bfloat16, jnp.float32, jnp.int32
     vmem = pl.BlockSpec(memory_space=pltpu.VMEM)
     any_space = pl.BlockSpec(memory_space=pl.ANY)
@@ -386,19 +472,20 @@
             pltpu.VMEM((kinds, 2 * sampled // LANES, LANES), bf16),
             pltpu.VMEM((16, edge_total), f32),
             pltpu.VMEM((16, edge_total), f32),
-            pltpu.VMEM((kinds, CORES * feat, cap), bf16),
+            pltpu.VMEM((2, kinds, cap, CORES * feat), bf16),
             pltpu.VMEM((MATS, SEEDS, cap), bf16),
-            pltpu.VMEM((MATS, SEEDS, CORES * feat), bf16),
-            pltpu.VMEM((items, kinds, SEEDS, half), f32),
-            pltpu.VMEM((items, planes, kinds, SEEDS, half), bf16),
-            pltpu.VMEM((items, planes, kinds, SEEDS, half), bf16),
-            pltpu.VMEM((items, CORES, kinds, SEEDS, quarter), bf16),
-            pltpu.VMEM((groups, kinds, SEEDS, quarter), bf16),
+            pltpu.VMEM((items, kinds, WAYS, planes, CORES, SEEDS // WAYS, quarter), bf16),
+            pltpu.VMEM((items, kinds, WAYS, planes, CORES, SEEDS // WAYS, quarter), bf16),
+            pltpu.VMEM((items, kinds, planes, CORES, SEEDS // WAYS, quarter), bf16),
+            pltpu.VMEM((items, kinds, WAYS, CORES, SEEDS // WAYS, quarter), bf16),
+            pltpu.VMEM((groups + (planes - 1) * CORES, kinds, WAYS, SEEDS // WAYS, quarter), bf16),
             dma((kinds + 1,)), dma((kinds + 1,)), dma((kinds + 1,)),
             dma((items,)), dma((items,)),
             dma((groups,)), dma((items, CORES)),
-            dma((items, planes, kinds)), dma((items, planes, kinds)),
-            dma((items, CORES, kinds)), dma((groups, kinds)),
+            dma((items, kinds, WAYS, planes)), dma((items, kinds, WAYS, planes)),
+            dma((items, kinds)), dma((items, kinds)),
+            dma((items, kinds, WAYS, CORES)), dma((groups, kinds, WAYS)),
+            dma((kinds, planes, CORES)), dma((kinds, planes, CORES)),
         ],
         compiler_params=pltpu.CompilerParams(
             collective_id=0, has_side_effects=True, vmem_limit_bytes=60 * 1024 * 1024),

time: 56.1 us -> 46.2 us (0.82)
  Pallas kernels: 54.4 us -> 44.4 us
    pallas_call x1, Pallas kernels: 54.4 us -> 44.4 us  [per_device(): pl.pallas_call(functools.partial(kernel, groups, shares), out_shape=jax.S...]
where the time goes in v2:
time: 46.2 us; the launch traced here: 46 us
  Pallas kernels  44.4 us (96%)
  local copies, waits for them, and re-layouts  1.54 us (3%)
    pallas_call x1, Pallas kernels, per_device(): pl.pallas_call(functools.partial(kernel, groups, shares), out_shape=jax.S...  44.4 us
    unnamed x1, local copies, waits for them, and re-layouts  1.54 us

profile of v2, /device:TPU:0, one launch (start us, length us, event | category | flops | bytes accessed | tf_op | source)
XLA Modules:
  0.0 46.0 jit_solution(15071736964391824337)
XLA Ops:
  0.0 44.4 %shard_map.73 = bf16[3,128,128]{2,1,0:T(8,128)(2,1)} custom-call(bf16[3,128,2048]{2,1,0:T(8,128)(2,1)} %features_in.1, bf16[11,128,512]{2,1,0:T(8,128)(2,1)} %weights_in.1, s32[3,1,2048]{2,1,0:T(1,128)} %bitcast.2, s32[3,2048]{1,0:T(4,128)} %row.1, s32[8,2048]{1,0:T(8,128)} %src.1, s32[8,2048]{1,0:T(8,128)} %dst.1, s32[1,8]{1,0:T(1,128)} %bitcast.3), custom_call_target="tpu_custom_call" | custom-call | tf_op jit(solution)/shard_map/pallas_call | solution.py:459
  44.4 1.5 %copy.9 = bf16[3,128,128]{2,1,0:T(8,128)(2,1)} copy(bf16[3,128,128]{2,1,0:T(8,128)(2,1)} %shard_map.73) | data formatting | bytes 196608

commit v3 on v2

--- a/solution.py
+++ b/solution.py
@@ -24,6 +24,7 @@
 SHARE = RELS // CORES
 STEP = 256
 LANES = 128
+ONE_HOT = jnp.float8_e4m3fn
 MESH = pl.DeviceIdType.MESH
 NT = (((1,), (1,)), ((), ()))
 
@@ -32,10 +33,10 @@
     return n.bit_length() - 1
 
 
-def kernel(groups, shares, features_in, weights_in, owner, row, src, dst, count, out,
-           feats, weights, iota, req_send, req_recv, info_send, info_recv, table,
+def kernel(groups, shares, features_in, weights_in, owner_in, row_in, src_in, dst_in, count, out,
+           owner, row, src, dst, feats, weights, req_send, req_recv, info_send, info_recv, table,
            lidx, ridx, picked, adj, xsend, xrecv, yrecv, zsend, zrecv,
-           in_sem, fx_ss, fx_rs, req_ss, req_rs, info_ss, info_rs, x_ss, x_rs, y_ss, y_rs, z_ss, z_rs, own_ss, own_rs):
+           in_sem, list_sem, fx_ss, fx_rs, req_ss, req_rs, info_ss, info_rs, x_ss, x_rs, y_ss, y_rs, z_ss, z_rs, own_ss, own_rs, near_ss, near_rs):
     kinds, _, feat, rows = feats.shape
     both = CORES * feat
     sampled = row.shape[1]
@@ -55,7 +56,6 @@
     core = lax.rem(m, CORES)
     plane = m // CORES
     f32, bf16, i32 = jnp.float32, jnp.bfloat16, jnp.int32
-    one, zero = jnp.ones((), bf16), jnp.zeros((), bf16)
 
     def at(group, mp):
         return {"dp": group, "mp": mp}
@@ -63,18 +63,27 @@
     def remote(source, target, ss, rs, group, mp):
         return pltpu.make_async_remote_copy(source, target, ss, rs, device_id=at(group, mp), device_id_type=MESH)
 
-    def hits(index, size):
-        n = index.shape[1]
-        return jnp.where(iota[:size, :n] == index.astype(f32).astype(bf16), one, zero)
+    def levels(size):
+        return lax.broadcasted_iota(i32, (size, LANES), 0).astype(f32).astype(bf16)
+
+    def hits(index, size, kind=bf16):
+        level = levels(size)
+        index = index.astype(f32).astype(bf16)
+        yes, no = jnp.ones((), kind), jnp.zeros((), kind)
+        return jnp.concatenate(
+            [jnp.where(level == index[:, base:base + LANES], yes, no)
+             for base in range(0, index.shape[1], LANES)], axis=1)
 
     mate = m - core + lax.rem(core + 1, CORES)
     loads, swaps = [], []
     for k in range(kinds):
-        loads.append(pltpu.make_async_copy(features_in.at[k], feats.at[k, core], in_sem.at[k]))
-        swaps.append(remote(features_in.at[k], feats.at[k, core], fx_ss.at[k], fx_rs.at[k], g, mate))
-    loads.append(pltpu.make_async_copy(weights_in, weights.at[core], in_sem.at[kinds]))
-    swaps.append(remote(weights_in, weights.at[core], fx_ss.at[kinds], fx_rs.at[kinds], g, mate))
-    for copy in loads:
+        loads.append(pltpu.make_async_copy(features_in.at[k], feats.at[k, 0], in_sem.at[k]))
+        swaps.append(remote(features_in.at[k], feats.at[k, 1], fx_ss.at[k], fx_rs.at[k], g, mate))
+    loads.append(pltpu.make_async_copy(weights_in, weights.at[0], in_sem.at[kinds]))
+    swaps.append(remote(weights_in, weights.at[1], fx_ss.at[kinds], fx_rs.at[kinds], g, mate))
+    lists = [pltpu.make_async_copy(source, target, list_sem.at[n]) for n, (source, target) in enumerate(
+        ((owner_in, owner), (row_in, row), (src_in, src), (dst_in, dst)))]
+    for copy in lists + loads:
         copy.start()
 
     barrier = pltpu.get_barrier_semaphore()
@@ -85,8 +94,12 @@
     for e in range(1, planes):
         pl.semaphore_signal(
             barrier, inc=1, device_id=at(g, lax.rem(plane + e, planes) * CORES + core), device_id_type=MESH)
-
-    iota[...] = lax.broadcasted_iota(i32, iota.shape, 0).astype(f32).astype(bf16)
+    pl.semaphore_wait(barrier, CORES * (groups - 1) + planes)
+    for copy in swaps:
+        copy.start()
+    for copy in lists:
+        copy.wait()
+
     tri = (lax.broadcasted_iota(i32, (STEP, STEP), 0) <= lax.broadcasted_iota(i32, (STEP, STEP), 1))
     tri = jnp.where(tri, 1.0, 0.0).astype(bf16)
     hot = jnp.concatenate([
@@ -102,10 +115,6 @@
         ranks.append((here + (carry - 1.0)) * piece)
         carry = carry + here[:, STEP - 1:]
     ranks = jnp.concatenate(ranks, axis=1)
-
-    pl.semaphore_wait(barrier, CORES * (groups - 1) + planes)
-    for copy in swaps:
-        copy.start()
 
     blocks = sampled // LANES
     parts = cap // LANES
@@ -193,51 +202,71 @@
     def info_wait(t, c):
         remote(info_send, info_recv.at[t, c], info_ss.at[0], info_rs.at[t, c], g, mate).wait_recv()
 
-    def x_copy(i, w, e, t):
+    def x_copy(i, w, e, t=slice(None)):
         to = lax.rem(plane + e, planes) * CORES + core
-        return remote(xsend.at[i, t, w, e], xrecv.at[i, t, w, e], x_ss.at[i, t, w, e], x_rs.at[i, t, w, e], g, to)
-
-    def y_copy(i, t):
-        return remote(xsend.at[i, t, 1], yrecv.at[i, t], y_ss.at[i, t], y_rs.at[i, t], g ^ 1, plane * CORES)
-
-    def z_copy(i, d, c, t, w):
-        return remote(zsend.at[i, t, w, c], zrecv.at[d, t, w], z_ss.at[i, t, w, c], z_rs.at[d, t, w],
+        return remote(xsend.at[i, t, w, e], xrecv.at[i, t, w, e], x_ss.at[i, w, e], x_rs.at[i, w, e], g, to)
+
+    def y_copy(i, t=slice(None)):
+        return remote(xsend.at[i, t, 1], yrecv.at[i, t], y_ss.at[i], y_rs.at[i], g ^ 1, plane * CORES)
+
+    def z_copy(i, d, w, c, t):
+        return remote(zsend.at[i, t, w, c], zrecv.at[d, t, w], z_ss.at[i, w], z_rs.at[d, w],
                       g ^ d, plane * CORES + c)
+
+    near = items - 2
+
+    def side(e):
+        return CORES * order(near) if e == 0 else groups + (planes - 1) * CORES + e - 1
+
+    def near_copy(e, c):
+        return remote(xsend.at[near, :, 1, e, c], zrecv.at[side(e), :, 1], near_ss.at[e, c], near_rs.at[e],
+                      g ^ (CORES * order(near)), lax.rem(plane + e, planes) * CORES + c)
+
+    def z_sent(i, w):
+        return remote(zsend.at[i, :, w], zsend.at[i, :, w], z_ss.at[i, w], z_rs.at[0, w], g, mate)
+
+    def z_landed(d, w):
+        return remote(zrecv.at[d, :, w], zrecv.at[d, :, w], z_ss.at[0, w], z_rs.at[d, w], g, mate)
 
     def far(e, d):
         return d if e == 0 else groups + (e - 1) * CORES + d
 
-    def own_copy(e, c, t, d):
-        return remote(xsend.at[items - 1, t, :, e, c], zrecv.at[far(e, d), t], own_ss.at[t, e, c], own_rs.at[t, e, d],
+    def own_copy(e, c, d, t=slice(None)):
+        return remote(xsend.at[items - 1, t, :, e, c], zrecv.at[far(e, d), t], own_ss.at[e, c], own_rs.at[e, d],
                       g ^ d, lax.rem(plane + e, planes) * CORES + c)
 
     def spot(i):
         return jnp.where(i < items - 2, i + 2, items - 1 - i)
 
     def merge(i):
+        y_copy(i).wait_recv()
         for n in range(kinds):
-            y_copy(i, n).wait_recv()
             for e in range(planes):
                 for c in range(CORES):
                     total = xsend[i, n, 1, e, c].astype(f32) + yrecv[i, n, e, c].astype(f32)
                     xsend[i, n, 1, e, c] = total.astype(bf16)
-            for e in range(1, planes):
-                x_copy(i, 1, e, n).start()
+        for e in reversed(range(planes)):
+            if isinstance(i, int) and i == near:
+                for c in range(CORES):
+                    near_copy(e, c).start()
+            elif e:
+                x_copy(i, 1, e).start()
 
     def deliver(i, w):
         d = CORES * spot(i) + core
+        for e in range(1, planes):
+            x_copy(i, w, e).wait_recv()
         for n in range(kinds):
-            for e in range(1, planes):
-                x_copy(i, w, e, n).wait_recv()
             for c in range(CORES):
                 total = xsend[i, n, w, 0, c].astype(f32)
                 for e in range(1, planes):
                     total = total + xrecv[i, n, w, e, c].astype(f32)
                 zsend[i, n, w, c] = total.astype(bf16)
-            for c in range(CORES):
-                z_copy(i, d, c, n, w).start()
-
-    def pick(t, where):
+        for c in range(CORES):
+            z_copy(i, d, w, c, slice(None)).start()
+
+    def pick(t, where, sides):
+        tall = len(sides) * feat
         for k in range(kinds):
             wanted = req_recv[t, k:k + 1, :cap]
             bank = wanted >> log2(low)
@@ -245,19 +274,17 @@
             choice = jnp.concatenate(
                 [hits(jnp.where((fine >= base) & (fine < base + STEP), fine - base, -1), STEP)
                  for base in range(0, low, STEP)], axis=0)
-            table_k = feats[k].reshape(both, rows)
-            table_k = jnp.concatenate([table_k[:, h * low:(h + 1) * low] for h in range(high)], axis=0)
-            found = jnp.dot(table_k, choice, preferred_element_type=f32)
-            chosen = found[:both]
+            rows_k = jnp.concatenate(
+                [feats[k, c, :, h * low:(h + 1) * low] for h in range(high) for c in sides], axis=0)
+            found = jnp.dot(rows_k, choice, preferred_element_type=f32)
+            chosen = found[:tall]
             for h in range(1, high):
-                chosen = jnp.where(bank == h, found[h * both:(h + 1) * both], chosen)
-            picked[where, k] = chosen.astype(bf16).T
+                chosen = jnp.where(bank == h, found[h * tall:(h + 1) * tall], chosen)
+            picked[where, k, :, sides[0] * feat:(sides[-1] + 1) * feat] = chosen.astype(bf16).T
 
     def build(place, ref_l, ref_r, n, width):
-        left = hits(ref_l[pl.ds(n, 1), :width], lo_n) if width <= STEP else jnp.concatenate(
-            [hits(ref_l[pl.ds(n, 1), base:base + STEP], lo_n) for base in range(0, width, STEP)], axis=1)
-        right = hits(ref_r[pl.ds(n, 1), :width], hi_n * SEEDS) if width <= STEP else jnp.concatenate(
-            [hits(ref_r[pl.ds(n, 1), base:base + STEP], hi_n * SEEDS) for base in range(0, width, STEP)], axis=1)
+        left = hits(ref_l[n:n + 1, :width], lo_n, ONE_HOT)
+        right = hits(ref_r[n:n + 1, :width], hi_n * SEEDS, ONE_HOT)
         counts = lax.dot_general(right, left, NT, preferred_element_type=f32).astype(bf16)
         for h in range(hi_n):
             adj[place, :, h * lo_n:(h + 1) * lo_n] = counts[h * SEEDS:(h + 1) * SEEDS]
@@ -267,7 +294,7 @@
         where = 1 if last else 0
         if not last:
             request_copy(t).wait_recv()
-            pick(t, 0)
+            pick(t, 0, range(CORES))
         if last:
             @pl.when(core > 0)
             def _():
@@ -318,11 +345,11 @@
                 for e in reversed(range(planes)):
                     for c in range(CORES):
                         if e or c:
-                            own_copy(e, c, n, core).start()
+                            own_copy(e, c, core, n).start()
 
                 @pl.when(core > 0)
                 def _():
-                    own_copy(0, 0, n, core).start()
+                    own_copy(0, 0, core, n).start()
 
                 @pl.when(core == 0)
                 def _():
@@ -341,27 +368,31 @@
         left = gather(0)
         make(groups_of[1][1])
         emit(0, left)
-        if not first:
+        def relay():
             @pl.when((i >= 2) & (core == 0))
             def _():
                 deliver(i - 2, 1)
 
+        def advance():
             @pl.when(core == 0)
             def _():
                 merge(i - 1)
 
             deliver(i - 1, 0)
+
+        if not first:
+            relay()
+        if not first and not last:
+            advance()
         for matrix in groups_of[1][2:] + groups_of[2][:1]:
             make(matrix)
         left = gather(1)
         for matrix in groups_of[2][1:]:
             make(matrix)
         emit(1, left)
+        if last:
+            advance()
         emit(2, gather(2))
-        if last:
-            @pl.when(core == 0)
-            def _():
-                deliver(i - 1, 1)
 
     def rest(i, _):
         item(i, False, False)
@@ -369,39 +400,48 @@
 
     for k in range(kinds):
         loads[k].wait()
-        swaps[k].wait()
 
     @pl.when(core > 0)
     def _():
         request_copy(0).wait_recv()
-    pick(0, 1)
+    pick(0, 1, (0,))
+    for k in range(kinds):
+        swaps[k].wait()
+    pick(0, 1, (1,))
     item(0, True, False)
     lax.fori_loop(1, items - 1, rest, 0)
     item(items - 1, False, True)
 
+    pieces = []
+    for i in range(items - 1):
+        for w in range(WAYS):
+            for c in range(CORES if w == 0 else 1):
+                d = CORES * order(i) + c
+                if w == 0 or i < near:
+                    z_landed(d, w).wait_recv()
+                    pieces.append((w, d))
+    for e in range(planes):
+        near_copy(e, 0).wait_recv()
+        pieces.append((1, side(e)))
+    for e in range(planes):
+        for d in range(CORES):
+            if e or d:
+                own_copy(e, 0, d).wait_recv()
+            else:
+                @pl.when(core > 0)
+                def _():
+                    own_copy(0, 0, 0).wait_recv()
+            for w in range(WAYS):
+                pieces.append((w, far(e, d)))
     for n in range(kinds):
         halves = []
         for w in range(WAYS):
             total = jnp.zeros((span, quarter), f32)
-            for i in range(items - 1):
-                for c in range(CORES if w == 0 else 1):
-                    d = CORES * order(i) + c
-                    z_copy(0, d, 0, n, w).wait_recv()
-                    total = total + zrecv[d, n, w].astype(f32)
+            for v, place in pieces:
+                if v == w:
+                    total = total + zrecv[place, n, w].astype(f32)
             halves.append(total)
-        for e in range(planes):
-            for d in range(CORES):
-                if e or d:
-                    own_copy(e, 0, n, d).wait_recv()
-                else:
-                    @pl.when(core > 0)
-                    def _():
-                        own_copy(0, 0, n, 0).wait_recv()
-                for w in range(WAYS):
-                    halves[w] = halves[w] + zrecv[far(e, d), n, w].astype(f32)
-        total = jnp.concatenate(halves, axis=0)
-        out[n] = jnp.maximum(total, 0.0).T.astype(bf16)
-
+        out[n] = jnp.maximum(jnp.concatenate(halves, axis=0), 0.0).T.astype(bf16)
     for t in range(items):
         if t == 0:
             @pl.when(core > 0)
@@ -414,34 +454,32 @@
         for c in range(1, CORES):
             info_copy(CORES * t + c).wait_send()
     for i in range(items - 1):
-        d = CORES * order(i) + core
-        for n in range(kinds):
-            for e in range(1, planes):
-                x_copy(i, 0, e, n).wait_send()
-            for c in range(CORES):
-                z_copy(i, d, c, n, 0).wait_send()
+        for e in range(1, planes):
+            x_copy(i, 0, e).wait_send()
+        z_sent(i, 0).wait_send()
 
         @pl.when(core == 0)
         def _():
-            for n in range(kinds):
+            if i < near:
                 for e in range(1, planes):
-                    x_copy(i, 1, e, n).wait_send()
-                for c in range(CORES):
-                    z_copy(i, d, c, n, 1).wait_send()
+                    x_copy(i, 1, e).wait_send()
+                z_sent(i, 1).wait_send()
+            else:
+                for e in range(planes):
+                    for c in range(CORES):
+                        near_copy(e, c).wait_send()
 
         @pl.when(core > 0)
         def _():
-            for n in range(kinds):
-                y_copy(i, n).wait_send()
-    for n in range(kinds):
-        for e in range(planes):
-            for c in range(CORES):
-                if e or c:
-                    own_copy(e, c, n, core).wait_send()
-
-        @pl.when(core > 0)
-        def _():
-            own_copy(0, 0, n, core).wait_send()
+            y_copy(i).wait_send()
+    for e in range(planes):
+        for c in range(CORES):
+            if e or c:
+                own_copy(e, c, core).wait_send()
+
+    @pl.when(core > 0)
+    def _():
+        own_copy(0, 0, core).wait_send()
 
 
 def per_device(features, weights, sample_owner, sample_row, edge_src, edge_dst, edge_count):
@@ -459,12 +497,15 @@
     return pl.pallas_call(
         functools.partial(kernel, groups, shares),
         out_shape=jax.ShapeDtypeStruct((kinds, quarter, SEEDS), bf16),
-        in_specs=[any_space] * 2 + [vmem] * 4 + [pl.BlockSpec(memory_space=pltpu.SMEM)],
+        in_specs=[any_space] * 6 + [pl.BlockSpec(memory_space=pltpu.SMEM)],
         out_specs=vmem,
         scratch_shapes=[
+            pltpu.VMEM((kinds, 1, sampled), i32),
+            pltpu.VMEM((kinds, sampled), i32),
+            pltpu.VMEM(edge_src.shape, i32),
+            pltpu.VMEM(edge_src.shape, i32),
             pltpu.VMEM((kinds, CORES, feat, rows), bf16),
             pltpu.VMEM((CORES, MATS, feat, width), bf16),
-            pltpu.VMEM((STEP, max(sampled, edge_total)), bf16),
             pltpu.VMEM((groups, kinds, cap + SEEDS), i32),
             pltpu.VMEM((items, kinds, cap + SEEDS), i32),
             pltpu.VMEM((SHARE, edge_total + SEEDS), i32),
@@ -478,14 +519,15 @@
             pltpu.VMEM((items, kinds, WAYS, planes, CORES, SEEDS // WAYS, quarter), bf16),
             pltpu.VMEM((items, kinds, planes, CORES, SEEDS // WAYS, quarter), bf16),
             pltpu.VMEM((items, kinds, WAYS, CORES, SEEDS // WAYS, quarter), bf16),
-            pltpu.VMEM((groups + (planes - 1) * CORES, kinds, WAYS, SEEDS // WAYS, quarter), bf16),
-            dma((kinds + 1,)), dma((kinds + 1,)), dma((kinds + 1,)),
+            pltpu.VMEM((groups + (planes - 1) * (CORES + 1), kinds, WAYS, SEEDS // WAYS, quarter), bf16),
+            dma((kinds + 1,)), dma((4,)), dma((kinds + 1,)), dma((kinds + 1,)),
             dma((items,)), dma((items,)),
             dma((groups,)), dma((items, CORES)),
-            dma((items, kinds, WAYS, planes)), dma((items, kinds, WAYS, planes)),
-            dma((items, kinds)), dma((items, kinds)),
-            dma((items, kinds, WAYS, CORES)), dma((groups, kinds, WAYS)),
-            dma((kinds, planes, CORES)), dma((kinds, planes, CORES)),
+            dma((items - 1, WAYS, planes)), dma((items - 1, WAYS, planes)),
+            dma((items - 1,)), dma((items - 1,)),
+            dma((items - 1, WAYS)), dma((groups, WAYS)),
+            dma((planes, CORES)), dma((planes, CORES)),
+            dma((planes, CORES)), dma((planes,)),
         ],
         compiler_params=pltpu.CompilerParams(
             collective_id=0, has_side_effects=True, vmem_limit_bytes=60 * 1024 * 1024),

time: 46.2 us -> 40.1 us (0.87)
  Pallas kernels: 44.4 us -> 38.4 us
    pallas_call x1, Pallas kernels: 44.4 us -> 38.4 us  [per_device(): pl.pallas_call(functools.partial(kernel, groups, shares), out_shape=jax.S...]
where the time goes in v3:
time: 40.1 us; the launch traced here: 39.9 us
  Pallas kernels  38.4 us (96%)
  local copies, waits for them, and re-layouts  1.54 us (4%)
    pallas_call x1, Pallas kernels, per_device(): pl.pallas_call(functools.partial(kernel, groups, shares), out_shape=jax.S...  38.4 us
    unnamed x1, local copies, waits for them, and re-layouts  1.54 us

profile of v3, /device:TPU:0, one launch (start us, length us, event | category | flops | bytes accessed | tf_op | source)
XLA Modules:
  0.0 39.9 jit_solution(4623699474011157956)
XLA Ops:
  0.0 38.4 %shard_map.73 = bf16[3,128,128]{2,1,0:T(8,128)(2,1)} custom-call(bf16[3,128,2048]{2,1,0:T(8,128)(2,1)} %features_in.1, bf16[11,128,512]{2,1,0:T(8,128)(2,1)} %weights_in.1, s32[3,1,2048]{2,1,0:T(1,128)} %bitcast.2, s32[3,2048]{1,0:T(4,128)} %row_in.1, s32[8,2048]{1,0:T(8,128)} %src_in.1, s32[8,2048]{1,0:T(8,128)} %dst_in.1, s32[1,8]{1,0:T(1,128)} %bitcast.3), custom_call_target="tpu_custom_call" | custom-call | tf_op jit(solution)/shard_map/pallas_call | solution.py:497
  38.4 1.5 %copy.9 = bf16[3,128,128]{2,1,0:T(8,128)(2,1)} copy(bf16[3,128,128]{2,1,0:T(8,128)(2,1)} %shard_map.73) | data formatting | bytes 196608

commit v4 on v3

--- a/solution.py
+++ b/solution.py
@@ -33,8 +33,8 @@
     return n.bit_length() - 1
 
 
-def kernel(groups, shares, features_in, weights_in, owner_in, row_in, src_in, dst_in, count, out,
-           owner, row, src, dst, feats, weights, req_send, req_recv, info_send, info_recv, table,
+def kernel(groups, shares, features_in, weights_in, owner_in, row_in, src_in, dst_in, count_in, out,
+           owner, row, src, dst, count, feats, weights, req_send, req_recv, info_send, info_recv, table,
            lidx, ridx, picked, adj, xsend, xrecv, yrecv, zsend, zrecv,
            in_sem, list_sem, fx_ss, fx_rs, req_ss, req_rs, info_ss, info_rs, x_ss, x_rs, y_ss, y_rs, z_ss, z_rs, own_ss, own_rs, near_ss, near_rs):
     kinds, _, feat, rows = feats.shape
@@ -82,7 +82,7 @@
     loads.append(pltpu.make_async_copy(weights_in, weights.at[0], in_sem.at[kinds]))
     swaps.append(remote(weights_in, weights.at[1], fx_ss.at[kinds], fx_rs.at[kinds], g, mate))
     lists = [pltpu.make_async_copy(source, target, list_sem.at[n]) for n, (source, target) in enumerate(
-        ((owner_in, owner), (row_in, row), (src_in, src), (dst_in, dst)))]
+        ((owner_in, owner), (row_in, row), (src_in, src), (dst_in, dst), (count_in, count)))]
     for copy in lists + loads:
         copy.start()
 
@@ -204,7 +204,7 @@
 
     def x_copy(i, w, e, t=slice(None)):
         to = lax.rem(plane + e, planes) * CORES + core
-        return remote(xsend.at[i, t, w, e], xrecv.at[i, t, w, e], x_ss.at[i, w, e], x_rs.at[i, w, e], g, to)
+        return remote(xsend.at[i, t, w, e], xrecv.at[i, t, w, e], x_ss.at[i, w, e - 1], x_rs.at[i, w, e - 1], g, to)
 
     def y_copy(i, t=slice(None)):
         return remote(xsend.at[i, t, 1], yrecv.at[i, t], y_ss.at[i], y_rs.at[i], g ^ 1, plane * CORES)
@@ -292,19 +292,15 @@
     def item(i, first, last):
         t = order(i) if first or last else spot(i)
         where = 1 if last else 0
-        if not last:
+        if first:
             request_copy(t).wait_recv()
             pick(t, 0, range(CORES))
-        if last:
-            @pl.when(core > 0)
-            def _():
-                info_wait(t, 0)
-        else:
-            info_wait(t, 0)
-        info_wait(t, 1)
-        if first:
+            for c in range(CORES):
+                info_wait(t, c)
             loads[kinds].wait()
             swaps[kinds].wait()
+        if not first and not last:
+            pick(t, 0, range(CORES))
         for c in range(CORES):
             packed = info_recv[t, c, :, :edge_total] - g * (cap * SEEDS)
             ok = (packed >= 0) & (packed < cap * SEEDS)
@@ -374,14 +370,14 @@
                 deliver(i - 2, 1)
 
         def advance():
+            relay()
+
             @pl.when(core == 0)
             def _():
                 merge(i - 1)
 
             deliver(i - 1, 0)
 
-        if not first:
-            relay()
         if not first and not last:
             advance()
         for matrix in groups_of[1][2:] + groups_of[2][:1]:
@@ -409,6 +405,15 @@
         swaps[k].wait()
     pick(0, 1, (1,))
     item(0, True, False)
+    for i in range(1, items - 1):
+        request_copy(order(i)).wait_recv()
+        for c in range(CORES):
+            info_wait(order(i), c)
+    info_wait(0, 1)
+
+    @pl.when(core > 0)
+    def _():
+        info_wait(0, 0)
     lax.fori_loop(1, items - 1, rest, 0)
     item(items - 1, False, True)
 
@@ -492,18 +497,19 @@
     quarter = width // shares
     bf16, f32, i32 = jnp.bfloat16, jnp.float32, jnp.int32
     vmem = pl.BlockSpec(memory_space=pltpu.VMEM)
-    any_space = pl.BlockSpec(memory_space=pl.ANY)
+    hbm = pl.BlockSpec(memory_space=pltpu.HBM)
     dma = pltpu.SemaphoreType.DMA
     return pl.pallas_call(
         functools.partial(kernel, groups, shares),
         out_shape=jax.ShapeDtypeStruct((kinds, quarter, SEEDS), bf16),
-        in_specs=[any_space] * 6 + [pl.BlockSpec(memory_space=pltpu.SMEM)],
+        in_specs=[hbm] * 7,
         out_specs=vmem,
         scratch_shapes=[
             pltpu.VMEM((kinds, 1, sampled), i32),
             pltpu.VMEM((kinds, sampled), i32),
             pltpu.VMEM(edge_src.shape, i32),
             pltpu.VMEM(edge_src.shape, i32),
+            pltpu.SMEM((1, RELS), i32),
             pltpu.VMEM((kinds, CORES, feat, rows), bf16),
             pltpu.VMEM((CORES, MATS, feat, width), bf16),
             pltpu.VMEM((groups, kinds, cap + SEEDS), i32),
@@ -520,18 +526,19 @@
             pltpu.VMEM((items, kinds, planes, CORES, SEEDS // WAYS, quarter), bf16),
             pltpu.VMEM((items, kinds, WAYS, CORES, SEEDS // WAYS, quarter), bf16),
             pltpu.VMEM((groups + (planes - 1) * (CORES + 1), kinds, WAYS, SEEDS // WAYS, quarter), bf16),
-            dma((kinds + 1,)), dma((4,)), dma((kinds + 1,)), dma((kinds + 1,)),
+            dma((kinds + 1,)), dma((5,)), dma((kinds + 1,)), dma((kinds + 1,)),
             dma((items,)), dma((items,)),
             dma((groups,)), dma((items, CORES)),
-            dma((items - 1, WAYS, planes)), dma((items - 1, WAYS, planes)),
+            dma((items - 1, WAYS, planes - 1)), dma((items - 1, WAYS, planes - 1)),
             dma((items - 1,)), dma((items - 1,)),
             dma((items - 1, WAYS)), dma((groups, WAYS)),
             dma((planes, CORES)), dma((planes, CORES)),
             dma((planes, CORES)), dma((planes,)),
         ],
         compiler_params=pltpu.CompilerParams(
-            collective_id=0, has_side_effects=True, vmem_limit_bytes=60 * 1024 * 1024),
-    )(features, weights, sample_owner.transpose(0, 2, 1), sample_row, edge_src, edge_dst, edge_count.T)
+            collective_id=0, has_side_effects=True, vmem_limit_bytes=48 * 1024 * 1024),
+    )(*[pltpu.with_memory_space_constraint(value, pltpu.HBM) for value in (
+        features, weights, sample_owner.transpose(0, 2, 1), sample_row, edge_src, edge_dst, edge_count.T)])
 
 
 def solution(mesh):

time: 40.1 us -> 36.7 us (0.915)
  Pallas kernels: 38.4 us -> 35.9 us
  local copies, waits for them, and re-layouts: 1.54 us -> 0.64 us
    pallas_call x1, Pallas kernels: 38.4 us -> 35.9 us  [per_device(): pl.pallas_call(functools.partial(kernel, groups, shares), out_shape=jax.S...]
    unnamed x1, local copies, waits for them, and re-layouts: 1.54 us -> 0.64 us
where the time goes in v4:
time: 36.7 us; the launch traced here: 36.6 us
  Pallas kernels  35.9 us (98%)
  local copies, waits for them, and re-layouts  0.64 us (2%)
    pallas_call x1, Pallas kernels, per_device(): pl.pallas_call(functools.partial(kernel, groups, shares), out_shape=jax.S...  35.9 us

profile of v4, /device:TPU:0, one launch (start us, length us, event | category | flops | bytes accessed | tf_op | source)
XLA Modules:
  0.0 36.6 jit_solution(6727129098672154685)
XLA Ops:
  0.0 35.9 %shard_map.73 = bf16[3,128,128]{2,1,0:T(8,128)(2,1)S(1)} custom-call(bf16[3,128,2048]{2,1,0:T(8,128)(2,1)} %features_in.1, bf16[11,128,512]{2,1,0:T(8,128)(2,1)} %weights_in.1, s32[3,1,2048]{2,1,0:T(1,128)} %bitcast.2, s32[3,2048]{1,0:T(4,128)} %row_in.1, s32[8,2048]{1,0:T(8,128)} %src_in.1, s32[8,2048]{1,0:T(8,128)} %dst_in.1, s32[1,8]{1,0:T(1,128)} %bitcast.3), custom_call_target="tpu_custom_call" | custom-call | tf_op jit(solution)/shard_map/pallas_call | solution.py:502
  35.9 0.6 %copy.9 = bf16[3,128,128]{2,1,0:T(8,128)(2,1)} copy(bf16[3,128,128]{2,1,0:T(8,128)(2,1)S(1)} %shard_map.73) | data formatting | bytes 196608

commit v5 on v4

--- a/solution.py
+++ b/solution.py
@@ -78,9 +78,9 @@
     loads, swaps = [], []
     for k in range(kinds):
         loads.append(pltpu.make_async_copy(features_in.at[k], feats.at[k, 0], in_sem.at[k]))
-        swaps.append(remote(features_in.at[k], feats.at[k, 1], fx_ss.at[k], fx_rs.at[k], g, mate))
+        swaps.append(remote(feats.at[k, 0], feats.at[k, 1], fx_ss.at[k], fx_rs.at[k], g, mate))
     loads.append(pltpu.make_async_copy(weights_in, weights.at[0], in_sem.at[kinds]))
-    swaps.append(remote(weights_in, weights.at[1], fx_ss.at[kinds], fx_rs.at[kinds], g, mate))
+    swaps.append(remote(weights.at[0], weights.at[1], fx_ss.at[kinds], fx_rs.at[kinds], g, mate))
     lists = [pltpu.make_async_copy(source, target, list_sem.at[n]) for n, (source, target) in enumerate(
         ((owner_in, owner), (row_in, row), (src_in, src), (dst_in, dst), (count_in, count)))]
     for copy in lists + loads:
@@ -94,9 +94,6 @@
     for e in range(1, planes):
         pl.semaphore_signal(
             barrier, inc=1, device_id=at(g, lax.rem(plane + e, planes) * CORES + core), device_id_type=MESH)
-    pl.semaphore_wait(barrier, CORES * (groups - 1) + planes)
-    for copy in swaps:
-        copy.start()
     for copy in lists:
         copy.wait()
 
@@ -118,14 +115,11 @@
 
     blocks = sampled // LANES
     parts = cap // LANES
+    places = []
     for k in range(kinds):
         mine = hot[k * groups:(k + 1) * groups]
         rank = jnp.sum(ranks[k * groups:(k + 1) * groups], axis=0, keepdims=True).astype(i32)
-        place = owner[k] * cap + rank
-        coarse = (place >> 8).astype(f32)
-        fine = (place & 255).astype(f32)
-        table[k] = jnp.concatenate(
-            [part[:, b * LANES:(b + 1) * LANES] for part in (coarse, fine) for b in range(blocks)], axis=0).astype(bf16)
+        places.append(owner[k] * cap + rank)
         wanted = row[k:k + 1, :]
         tall = mine * (wanted >> 8).astype(f32)
         wide = mine * (wanted & 255).astype(f32)
@@ -140,6 +134,12 @@
                 req_send[o, k:k + 1, h * LANES:(h + 1) * LANES] = listed[h * groups + o:h * groups + o + 1]
             req_send[o, k:k + 1, cap:] = seeds[o:o + 1]
 
+    for copy in loads:
+        copy.wait()
+    pl.semaphore_wait(barrier, CORES * (groups - 1) + planes)
+    for copy in swaps:
+        copy.start()
+
     def order(i):
         return i + 2 if i < items - 2 else items - 1 - i
 
@@ -160,6 +160,11 @@
         else:
             request_copy(t).start()
 
+    for k in range(kinds):
+        coarse = (places[k] >> 8).astype(f32)
+        fine = (places[k] & 255).astype(f32)
+        table[k] = jnp.concatenate(
+            [part[:, b * LANES:(b + 1) * LANES] for part in (coarse, fine) for b in range(blocks)], axis=0).astype(bf16)
     slots = lax.broadcasted_iota(i32, (1, edge_total), 1)
     banks = lax.broadcasted_iota(i32, (blocks, edge_total), 0)
     ones8 = jnp.ones((8, LANES), bf16)
@@ -297,7 +302,6 @@
             pick(t, 0, range(CORES))
             for c in range(CORES):
                 info_wait(t, c)
-            loads[kinds].wait()
             swaps[kinds].wait()
         if not first and not last:
             pick(t, 0, range(CORES))
@@ -386,16 +390,13 @@
         for matrix in groups_of[2][1:]:
             make(matrix)
         emit(1, left)
+        emit(2, gather(2))
         if last:
             advance()
-        emit(2, gather(2))
 
     def rest(i, _):
         item(i, False, False)
         return 0
-
-    for k in range(kinds):
-        loads[k].wait()
 
     @pl.when(core > 0)
     def _():

time: 36.7 us -> 36.8 us (level)
  no operation moved by 1% of the time
where the time goes in v5:
time: 36.8 us; the launch traced here: 36.7 us
  Pallas kernels  36.1 us (98%)
  local copies, waits for them, and re-layouts  0.64 us (2%)
    pallas_call x1, Pallas kernels, per_device(): pl.pallas_call(functools.partial(kernel, groups, shares), out_shape=jax.S...  36.1 us

profile of v5, /device:TPU:0, one launch (start us, length us, event | category | flops | bytes accessed | tf_op | source)
XLA Modules:
  0.0 36.7 jit_solution(11360115734194858852)
XLA Ops:
  0.0 36.1 %shard_map.73 = bf16[3,128,128]{2,1,0:T(8,128)(2,1)S(1)} custom-call(bf16[3,128,2048]{2,1,0:T(8,128)(2,1)} %features_in.1, bf16[11,128,512]{2,1,0:T(8,128)(2,1)} %weights_in.1, s32[3,1,2048]{2,1,0:T(1,128)} %bitcast.2, s32[3,2048]{1,0:T(4,128)} %row_in.1, s32[8,2048]{1,0:T(8,128)} %src_in.1, s32[8,2048]{1,0:T(8,128)} %dst_in.1, s32[1,8]{1,0:T(1,128)} %bitcast.3), custom_call_target="tpu_custom_call" | custom-call | tf_op jit(solution)/shard_map/pallas_call | solution.py:503
  36.1 0.6 %copy.9 = bf16[3,128,128]{2,1,0:T(8,128)(2,1)} copy(bf16[3,128,128]{2,1,0:T(8,128)(2,1)S(1)} %shard_map.73) | data formatting | bytes 196608

commit v6 on v4

--- a/solution.py
+++ b/solution.py
@@ -118,14 +118,11 @@
 
     blocks = sampled // LANES
     parts = cap // LANES
+    places = []
     for k in range(kinds):
         mine = hot[k * groups:(k + 1) * groups]
         rank = jnp.sum(ranks[k * groups:(k + 1) * groups], axis=0, keepdims=True).astype(i32)
-        place = owner[k] * cap + rank
-        coarse = (place >> 8).astype(f32)
-        fine = (place & 255).astype(f32)
-        table[k] = jnp.concatenate(
-            [part[:, b * LANES:(b + 1) * LANES] for part in (coarse, fine) for b in range(blocks)], axis=0).astype(bf16)
+        places.append(owner[k] * cap + rank)
         wanted = row[k:k + 1, :]
         tall = mine * (wanted >> 8).astype(f32)
         wide = mine * (wanted & 255).astype(f32)
@@ -160,6 +157,11 @@
         else:
             request_copy(t).start()
 
+    for k in range(kinds):
+        coarse = (places[k] >> 8).astype(f32)
+        fine = (places[k] & 255).astype(f32)
+        table[k] = jnp.concatenate(
+            [part[:, b * LANES:(b + 1) * LANES] for part in (coarse, fine) for b in range(blocks)], axis=0).astype(bf16)
     slots = lax.broadcasted_iota(i32, (1, edge_total), 1)
     banks = lax.broadcasted_iota(i32, (blocks, edge_total), 0)
     ones8 = jnp.ones((8, LANES), bf16)
@@ -386,9 +388,9 @@
         for matrix in groups_of[2][1:]:
             make(matrix)
         emit(1, left)
+        emit(2, gather(2))
         if last:
             advance()
-        emit(2, gather(2))
 
     def rest(i, _):
         item(i, False, False)

time: 36.7 us -> 36.6 us (level)
  no operation moved by 1% of the time
where the time goes in v6:
time: 36.6 us; the launch traced here: 36.5 us
  Pallas kernels  35.8 us (98%)
  local copies, waits for them, and re-layouts  0.64 us (2%)
    pallas_call x1, Pallas kernels, per_device(): pl.pallas_call(functools.partial(kernel, groups, shares), out_shape=jax.S...  35.8 us

profile of v6, /device:TPU:0, one launch (start us, length us, event | category | flops | bytes accessed | tf_op | source)
XLA Modules:
  0.0 36.5 jit_solution(4224567418207709136)
XLA Ops:
  0.0 35.8 %shard_map.73 = bf16[3,128,128]{2,1,0:T(8,128)(2,1)S(1)} custom-call(bf16[3,128,2048]{2,1,0:T(8,128)(2,1)} %features_in.1, bf16[11,128,512]{2,1,0:T(8,128)(2,1)} %weights_in.1, s32[3,1,2048]{2,1,0:T(1,128)} %bitcast.2, s32[3,2048]{1,0:T(4,128)} %row_in.1, s32[8,2048]{1,0:T(8,128)} %src_in.1, s32[8,2048]{1,0:T(8,128)} %dst_in.1, s32[1,8]{1,0:T(1,128)} %bitcast.3), custom_call_target="tpu_custom_call" | custom-call | tf_op jit(solution)/shard_map/pallas_call | solution.py:504
  35.8 0.6 %copy.9 = bf16[3,128,128]{2,1,0:T(8,128)(2,1)} copy(bf16[3,128,128]{2,1,0:T(8,128)(2,1)S(1)} %shard_map.73) | data formatting | bytes 196608
